TPU v7x, 32 devices: a whole 2x2x4 slice. The times are simulated.
32 devices in a mesh: ty: 4 (over y, x), tx: 8 (over z, core).
Axes of the slice: x: 2, y: 2, z: 4, core: 2. Of those that a mesh axis runs over, the one named last changes fastest.
Arguments:
- surface_levels: float32 [512, 16384], P('ty', 'tx'), may hold values from -6 to 6
- bearing_index: int32 [4], replicated, may hold values from 0 to 15
- stencil_displacements: int32 [4], replicated, may hold values from -4 to 4
- camera_altitude_class: int32 [4], replicated, may hold values from 0 to 3
Outputs:
- margin: float32 [4, 512, 16384], P(None, 'ty', 'tx')
Inputs may be any that keep to these rules, and one draw needn't show every extreme that they name: `bearing_index`: azimuth indices.
All inputs are finite; a program needn't handle non-finite values.
Results may differ from a plain program's by a relative error of at most 0.00002.
Values sent between devices are 32-bit elements; how exact they have to be, the bound alone decides.
No kernel may reach another device: no remote copies, remote signals or barrier semaphores. Data moves between devices by JAX's collectives and lax.ppermute only.
A program may use at most 192 MiB of HBM per device.

v0:
```python
import math

import jax
import jax.numpy as jnp
from jax import lax
from jax.sharding import PartitionSpec as P

AZIMUTHS = 4
STENCIL_REACH = 4


def padded(cells, sides, width):
    for axis, dim in sides:
        count = lax.axis_size(axis)
        ends = count - 1
        head = lax.slice_in_dim(cells, 0, width, axis=dim)
        tail = lax.slice_in_dim(cells, cells.shape[dim] - width, cells.shape[dim], axis=dim)
        cells = jnp.concatenate(
            [
                lax.ppermute(tail, axis, [(i, (i + 1) % count) for i in range(ends)]),
                cells,
                lax.ppermute(head, axis, [((i + 1) % count, i) for i in range(ends)]),
            ],
            axis=dim,
        )
    return cells


def prefix(part, axis, combine, identity):
    place = lax.axis_index(axis)
    gathered = lax.all_gather(part, axis)
    state = jnp.zeros_like(part) + jnp.asarray(identity, part.dtype)

    def one(hop, state):
        return combine(state, lax.dynamic_index_in_dim(gathered, hop, 0, False))

    return lax.fori_loop(0, place, one, state)


def view_tables(bearing_index, camera_altitude_class, easting_span):
    angle_idx = bearing_index.astype(jnp.float32)
    frac = ((bearing_index * 5 % 16).astype(jnp.float32) + 0.5) / 16.0
    theta = (angle_idx - 7.5) * (math.pi / 32.0)
    stride = 1.0 / jnp.cos(theta)
    slope = (1.0 + camera_altitude_class.astype(jnp.float32)) / (4.0 * easting_span)
    cube = frac * frac * frac
    square = frac * frac
    weights = jnp.stack(
        [
            (-cube + 2.0 * square - frac) / 2.0,
            (3.0 * cube - 5.0 * square + 2.0) / 2.0,
            (-3.0 * cube + 4.0 * square + frac) / 2.0,
            (cube - square) / 2.0,
        ],
        axis=1,
    )
    return (weights, stride * slope)


def on_device(surface_levels, bearing_index, stencil_displacements, camera_altitude_class):
    northing_extent, easting_extent = surface_levels.shape
    easting_span = easting_extent * lax.axis_size("tx")
    weights, rise = view_tables(bearing_index, camera_altitude_class, easting_span)
    bordered_surface = padded(surface_levels, (("ty", 0),), STENCIL_REACH + 2)
    first_col = lax.axis_index("tx") * easting_extent
    columns = (first_col + jnp.arange(easting_extent)).astype(jnp.float32)
    stacked = []
    for which in range(AZIMUTHS):
        strips = jnp.zeros((northing_extent, easting_extent), jnp.float32)
        for tap_index in range(4):
            start = stencil_displacements[which] + tap_index + STENCIL_REACH + 1
            strips = strips + weights[which, tap_index] * lax.dynamic_slice_in_dim(
                bordered_surface, start, northing_extent, 0
            )
        stacked.append(strips + rise[which] * columns[None, :])
    lifted = jnp.stack(stacked, axis=0)
    running = lax.cummax(lifted, axis=2)
    row_peak = running[:, :, -1]
    before = prefix(row_peak, "tx", jnp.maximum, jnp.full_like(row_peak, -jnp.inf))
    lowest = jnp.full((AZIMUTHS, northing_extent, 1), -jnp.inf, jnp.float32)
    earlier = jnp.concatenate([lowest, running[:, :, :-1]], axis=2)
    horizon = jnp.maximum(earlier, before[:, :, None])
    margin = jnp.maximum(horizon - lifted, 0.0)
    return margin


def solution(mesh):
    return jax.shard_map(
        on_device,
        mesh=mesh,
        in_specs=(P("ty", "tx"), P(), P(), P()),
        out_specs=P(None, "ty", "tx"),
        check_vma=False,
    )
```

profile of v0, /device:TPU:13, one launch (start us, length us, event | category | flops | bytes accessed | tf_op | source)
XLA Modules:
  0.0 88.7 jit_solution(15927352842759465589)
XLA Ops:
  0.0 0.9 fusion.15
  0.9 3.1 %collective-permute-start = (f32[6,2048]{1,0:T(8,128)S(1)}, f32[6,2048]{1,0:T(8,128)S(1)}, u32[]{:S(2)}, u32[]{:S(2)}) collective-permute-start(f32[6,2048]{1,0:T(8,128)S(1)} %get-tuple-element.43), channel_id=1, source_target_pairs={{0,8},{8,16},{16,24},{1,9},{9,17},{17,25},{2,10},{10,18},{18,26},{... | collective-permute-start | bytes 147464 | tf_op jit(solution)/shard_map/ppermute | solution.py:20
  4.0 3.1 %collective-permute-start.1 = (f32[6,2048]{1,0:T(8,128)S(1)}, f32[6,2048]{1,0:T(8,128)S(1)}, u32[]{:S(2)}, u32[]{:S(2)}) collective-permute-start(f32[6,2048]{1,0:T(8,128)S(1)} %get-tuple-element.44), channel_id=1, source_target_pairs={{8,0},{16,8},{24,16},{9,1},{17,9},{25,17},{10,2},{18,10},{26,18},{... | collective-permute-start | bytes 147464 | tf_op jit(solution)/shard_map/ppermute | solution.py:22
  7.1 1.5 %fusion.21 = (s32[1]{0:T(128)}, s32[1]{0:T(128)}, s32[1]{0:T(128)}, s32[1]{0:T(128)}) fusion(s32[4]{0:T(128)} %param.8), kind=kLoop, calls=%fused_computation.43 | loop fusion | bytes 32 | tf_op jit(solution)/shard_map/slice | solution.py:71
  8.6 0.8 subtract_multiply_fusion.1
  9.3 0.7 fusion.16
  10.0 0.6 convert_multiply_fusion.1
  10.7 0.6 convert_multiply_fusion.3
  11.2 0.6 fusion.19
  11.8 0.6 convert_multiply_fusion
  12.5 0.7 fusion.17
  13.2 0.6 convert_multiply_fusion.2
  24.5 1.6 %copy.19 = f32[128,2048]{0,1:T(8,128)S(1)} copy(f32[128,2048]{1,0:T(8,128)} %param.6) | data formatting | bytes 2097152 | tf_op args[0]
  36.1 0.0 collective-permute-done
  36.1 0.4 copy.18
  36.5 0.0 collective-permute-done.1
  36.5 0.4 copy.20
  36.9 0.9 pad_maximum_fusion
  37.8 8.0 %add_add_fusion.3 = (f32[128,2048]{0,1:T(8,128)S(1)}, f32[128,2048]{0,1:T(8,128)S(1)}) fusion(f32[140,2048]{0,1:T(8,128)S(1)} %pad_maximum_fusion, s32[]{:T(128)S(6)} %select_n.63, s32[]{:T(128)S(6)} %select_n.62, s32[]{:T(128)S(6)} %select_n.61, s32[]{:T(128)S(6)} %select_n.60, f32[2048]{0:T(1024)S(1)} %convert_multiply_fusion.3, f32[]{:T(128)} %bitcast.10, ...), kind=kLoop, calls=%fused_computation.16 | loop fusion | flops 4194304 | bytes 10502208 | tf_op jit(solution)/shard_map/add | solution.py:75
  45.7 0.6 copy.21
  46.3 0.6 copy.23
  47.0 8.0 %add_add_fusion.2 = (f32[128,2048]{0,1:T(8,128)S(1)}, f32[128,2048]{0,1:T(8,128)S(1)}) fusion(f32[140,2048]{0,1:T(8,128)S(1)} %pad_maximum_fusion, s32[]{:T(128)S(6)} %select_n.67, s32[]{:T(128)S(6)} %select_n.66, s32[]{:T(128)S(6)} %select_n.65, s32[]{:T(128)S(6)} %select_n.64, f32[2048]{0:T(1024)S(1)} %convert_multiply_fusion.2, f32[]{:T(128)} %bitcast.24, ...), kind=kLoop, calls=%fused_computation.15 | loop fusion | flops 4194304 | bytes 10502208 | tf_op jit(solution)/shard_map/add | solution.py:75
  54.9 0.0 copy-start.2
  54.9 0.6 copy.22
  55.6 0.3 copy-done.2
  55.9 0.6 copy.24
  56.5 0.3 fusion
  56.8 0.0 copy-start
  56.8 2.0 %copy-done = f32[4,128,16,128]{1,2,3,0:T(8,128)} copy-done((f32[4,128,16,128]{1,2,3,0:T(8,128)}, f32[4,128,16,128]{1,2,3,0:T(8,128)S(1)}, u32[]{:S(2)}) %copy-start) | copy-done | bytes 4194328
  58.9 2.6 %broadcast_maximum_fusion = f32[4,128,16,128]{1,2,3,0:T(8,128)S(1)} fusion(f32[4,128,16,128]{1,2,3,0:T(8,128)} %copy-done, f32[4,128,16]{1,2,0:T(8,128)S(1)} %slice.149), kind=kLoop, calls=%fused_computation.12 | loop fusion | flops 1048576 | bytes 8421376 | tf_op jit(solution)/shard_map/reduce_window_max | solution.py:77
  61.5 1.3 %copy.25 = f32[4,128,16,128]{1,3,2,0:T(8,128)S(1)} copy(f32[4,128,16,128]{1,2,3,0:T(8,128)S(1)} %broadcast_maximum_fusion) | data formatting | bytes 8388608 | tf_op jit(solution)/shard_map/reduce_window_max | solution.py:77
  62.8 0.0 copy-start.1
  62.8 2.0 %copy-done.1 = f32[4,128,16,128]{1,3,2,0:T(8,128)} copy-done((f32[4,128,16,128]{1,3,2,0:T(8,128)}, f32[4,128,16,128]{1,3,2,0:T(8,128)S(1)}, u32[]{:S(2)}) %copy-start.1) | copy-done | bytes 4194328
  64.8 14.1 %all-gather = f32[32,128,1]{1,2,0:T(1,128)S(1)} all-gather(f32[4,128,1]{1,2,0:T(1,128)S(1)} %slice.151), channel_id=2, replica_groups=mesh['ty'=4,'tx'=8] {'tx'}, dimensions={0}, use_global_device_ids=true | all-gather | bytes 18432 | tf_op jit(solution)/shard_map/all_gather | solution.py:31
  78.9 0.1 while.10
  79.0 4.3 %fusion.8 = f32[4,128,2048]{1,2,0:T(8,128)} fusion(f32[1,128,2048]{1,2,0:T(8,128)} %bitcast.78, f32[1,128,2048]{1,2,0:T(8,128)S(1)} %bitcast.74, f32[1,128,2048]{1,2,0:T(8,128)S(1)} %bitcast.76, f32[1,128,2048]{1,2,0:T(8,128)S(1)} %bitcast.72, f32[4,128,2047]{1,2,0:T(8,128)} %bitcast.70, f32[4,128]{1,0:T(4,128)S(1)} %get-tuple-element.28), kind=kLoop, calls=%fused_computation.10 | loop fusion | flops 6291456 | bytes 12582912 | tf_op jit(solution)/shard_map/max | solution.py:83
  83.3 5.3 %copy.26 = f32[4,128,2048]{2,1,0:T(8,128)} copy(f32[4,128,2048]{1,2,0:T(8,128)} %fusion.8) | data formatting | bytes 8388608 | tf_op jit(solution)/shard_map/max | solution.py:83
  (9 shorter events, 0.1 us)
Async XLA Ops:
  0.9 35.2 %collective-permute-start = (f32[6,2048]{1,0:T(8,128)S(1)}, f32[6,2048]{1,0:T(8,128)S(1)}, u32[]{:S(2)}, u32[]{:S(2)}) collective-permute-start(f32[6,2048]{1,0:T(8,128)S(1)} %get-tuple-element.43), channel_id=1, source_target_pairs={{0,8},{8,16},{16,24},{1,9},{9,17},{17,25},{2,10},{10,18},{18,26},{... | collective-permute-start | bytes 147464 | tf_op jit(solution)/shard_map/ppermute | solution.py:20
  4.0 32.5 %collective-permute-start.1 = (f32[6,2048]{1,0:T(8,128)S(1)}, f32[6,2048]{1,0:T(8,128)S(1)}, u32[]{:S(2)}, u32[]{:S(2)}) collective-permute-start(f32[6,2048]{1,0:T(8,128)S(1)} %get-tuple-element.44), channel_id=1, source_target_pairs={{8,0},{16,8},{24,16},{9,1},{17,9},{25,17},{10,2},{18,10},{26,18},{... | collective-permute-start | bytes 147464 | tf_op jit(solution)/shard_map/ppermute | solution.py:22
  54.9 1.0 %copy-start.2 = (f32[128,2048]{0,1:T(8,128)}, f32[128,2048]{0,1:T(8,128)S(1)}, u32[]{:S(2)}) copy-start(f32[128,2048]{0,1:T(8,128)S(1)} %get-tuple-element.42) | copy-start | bytes 3145732
  56.8 2.0 %copy-start = (f32[4,128,16,128]{1,2,3,0:T(8,128)}, f32[4,128,16,128]{1,2,3,0:T(8,128)S(1)}, u32[]{:S(2)}) copy-start(f32[4,128,16,128]{1,2,3,0:T(8,128)S(1)} %fusion) | copy-start | bytes 12582916
  62.8 2.0 %copy-start.1 = (f32[4,128,16,128]{1,3,2,0:T(8,128)}, f32[4,128,16,128]{1,3,2,0:T(8,128)S(1)}, u32[]{:S(2)}) copy-start(f32[4,128,16,128]{1,3,2,0:T(8,128)S(1)} %copy.25) | copy-start | bytes 12582916
where the time goes:
time: 89.5 us; the launch traced here: 88.7 us
  other arithmetic  27.4 us (31%)
  between operations  20.9 us (23%)
  local copies, waits for them, and re-layouts  20 us (22%)
  blocking collectives  14.1 us (16%)
  starting transfers between devices  6.18 us (7%)
    add x2, other arithmetic, on_device(): stacked.append(strips + rise[which] * columns[None, :])  15.9 us
    all_gather x1, blocking collectives, prefix(): gathered = lax.all_gather(part, axis)  14.1 us
    unnamed x7, local copies, waits for them, and re-layouts  5.9 us
    max x1, local copies, waits for them, and re-layouts, on_device(): margin = jnp.maximum(horizon - lifted, 0.0)  5.34 us
    max x1, other arithmetic, on_device(): margin = jnp.maximum(horizon - lifted, 0.0)  4.33 us
    ppermute x1, starting transfers between devices, padded(): lax.ppermute(tail, axis, [(i, (i + 1) % count) for i in range(ends)])  3.12 us
    ppermute x1, starting transfers between devices, padded(): lax.ppermute(head, axis, [((i + 1) % count, i) for i in range(ends)])  3.06 us
    another operation x1, other arithmetic, on_device(): running = lax.cummax(lifted, axis=2)  2.62 us
  transfers between devices with their start and end apart: 2, of which 0 were waited for; matrix products, arithmetic and copies ran while one was open for 10% of the time, Pallas kernels for 0%

commit v1 on v0

v1 whole, which is shorter than its diff:
```python
import functools
import math

import jax
import jax.numpy as jnp
from jax import lax
from jax.experimental import pallas as pl
from jax.experimental.pallas import tpu as pltpu
from jax.sharding import PartitionSpec as P

TAPS = 4
SUB = 8
LANE = 128
MIB = 1 << 20


def view_terms(bearing_ref, class_ref, which, easting_span):
    bearing = bearing_ref[which]
    frac = (lax.rem(bearing * 5, 16).astype(jnp.float32) + 0.5) * 0.0625
    theta = (bearing.astype(jnp.float32) - 7.5) * (math.pi / 32.0)
    stride = 1.0 / jnp.cos(jnp.full((SUB, LANE), theta, jnp.float32))
    slope = (1.0 + class_ref[which].astype(jnp.float32)) * (1.0 / (4.0 * easting_span))
    cube = frac * frac * frac
    square = frac * frac
    weights = (
        (-cube + 2.0 * square - frac) * 0.5,
        (3.0 * cube - 5.0 * square + 2.0) * 0.5,
        (-3.0 * cube + 4.0 * square + frac) * 0.5,
        (cube - square) * 0.5,
    )
    return weights, stride * slope


def column_tile(first_col, block):
    lane = lax.broadcasted_iota(jnp.int32, (SUB, LANE), 1)
    return (lane + (first_col + block * LANE)).astype(jnp.float32)


def lifted_tile(weights, ramp, rows_at):
    total = weights[0] * rows_at(0)
    for tap in range(1, TAPS):
        total = total + weights[tap] * rows_at(tap)
    return total + ramp


def scan_tiles(source, work, blocks):
    lane = lax.broadcasted_iota(jnp.int32, (SUB, LANE), 1)
    tiles = source
    step = 1
    while step < LANE:
        mask = lane < step
        for get, put in tiles(step):
            values = [get(j) for j in range(blocks)]
            rolled = [pltpu.roll(v, step, 1) for v in values]
            for j in range(blocks):
                before = rolled[j - 1] if j else jnp.full((SUB, LANE), -jnp.inf, jnp.float32)
                put(j, jnp.maximum(values[j], jnp.where(mask, before, rolled[j])))
        step *= 2


def inner_kernel(bearing_ref, disp_ref, class_ref, x_ref, lifted_ref, margin_ref, edge_ref, peak_ref, own, work, sems, *, tx):
    rows, cols = x_ref.shape
    blocks, tiles = cols // LANE, rows // SUB
    views = bearing_ref.shape[0]
    copies = [
        pltpu.make_async_copy(x_ref.at[:, pl.ds(j * LANE, LANE)], own.at[j], sems.at[j])
        for j in range(blocks)
    ]
    for copy in copies:
        copy.start()
    first_col = lax.axis_index("tx") * cols
    terms = [view_terms(bearing_ref, class_ref, k, cols * tx) for k in range(views)]
    for copy in copies:
        copy.wait()
    for j in range(blocks):
        edge_ref[0, j] = own[j, 0 : 2 * SUB, :]
        edge_ref[1, j] = own[j, rows - 2 * SUB : rows, :]
    for which in range(views):
        weights, rise = terms[which]
        disp = disp_ref[which] - 1
        ramps = [rise * column_tile(first_col, j) for j in range(blocks)]

        @pl.loop(1, tiles - 1)
        def _(t):
            for j in range(blocks):
                lifted_ref[which, t, j] = lifted_tile(
                    weights, ramps[j], lambda tap: own[j, pl.ds(t * SUB + disp + tap, SUB), :]
                )

        def stages(step):
            for t in range(1, tiles - 1):
                yield (
                    (lambda j, t=t: lifted_ref[which, t, j]) if step == 1 else (lambda j, t=t: work[t, j]),
                    functools.partial(put_tile, work, t),
                )

        scan_tiles(stages, None, blocks)
        for t in range(1, tiles - 1):
            peak = None
            for j in range(blocks):
                peak = work[t, j] if peak is None else jnp.maximum(peak, work[t, j])
                margin_ref[which, t, j] = peak - lifted_ref[which, t, j]
            peak_ref[which, t] = peak


def put_tile(ref, t, j, value):
    ref[t, j] = value


def edge_kernel(bearing_ref, disp_ref, class_ref, up_ref, down_ref, edge_ref, peak_ref, lifted_ref, sent_ref, ring, tall, *, tx, ty):
    cols = up_ref.shape[1]
    blocks = cols // LANE
    views, tiles = peak_ref.shape[:2]
    place = lax.axis_index("ty")
    first_col = lax.axis_index("tx") * cols
    for j in range(blocks):
        span = slice(j * LANE, (j + 1) * LANE)
        ring[0, j, 0:SUB, :] = jnp.where(place == 0, 0.0, up_ref[:, span])
        ring[0, j, SUB : 3 * SUB, :] = edge_ref[0, j]
        ring[1, j, 0 : 2 * SUB, :] = edge_ref[1, j]
        ring[1, j, 2 * SUB : 3 * SUB, :] = jnp.where(place == ty - 1, 0.0, down_ref[:, span])
    for which in range(views):
        weights, rise = view_terms(bearing_ref, class_ref, which, cols * tx)
        disp = disp_ref[which] - 1
        tops = []
        for end in range(2):
            top = None
            for j in range(blocks):
                value = lifted_tile(
                    weights,
                    rise * column_tile(first_col, j),
                    lambda tap: ring[end, j, pl.ds(SUB + disp + tap, SUB), :],
                )
                lifted_ref[which, end, j] = value
                top = value if top is None else jnp.maximum(top, value)
            tops.append(top)
        tall[0:SUB, :] = tops[0]
        for t in range(1, tiles - 1):
            tall[t * SUB : (t + 1) * SUB, :] = peak_ref[which, t]
        tall[(tiles - 1) * SUB : tiles * SUB, :] = tops[1]
        peaks = jnp.max(jnp.transpose(tall[...]), axis=0, keepdims=True)
        for i in range(tx):
            sent_ref[i, which : which + 1, :] = peaks


def final_kernel(got_ref, lifted_ref, margin_ref, edge_ref, out_ref, stage, work, tall, sems, *, tx):
    views, rows, cols = out_ref.shape
    blocks, tiles = cols // LANE, rows // SUB
    place = lax.axis_index("tx")
    before = jnp.full((views, rows), -jnp.inf, jnp.float32)
    for i in range(tx):
        before = jnp.maximum(before, jnp.where(i < place, got_ref[i], -jnp.inf))
    for which in range(views):
        tall[which] = jnp.transpose(jnp.broadcast_to(before[which : which + 1, :], (LANE, rows)))
    copies = []
    for which in range(views):

        @pl.loop(1, tiles - 1)
        def _(t):
            top = tall[which, pl.ds(t * SUB, SUB), :]
            for j in range(blocks):
                stage[which, pl.ds(t * SUB, SUB), j * LANE : (j + 1) * LANE] = jnp.maximum(
                    margin_ref[which, t, j], top - lifted_ref[which, t, j]
                )

        inner = pl.ds(SUB, rows - 2 * SUB)
        copies.append(pltpu.make_async_copy(stage.at[which, inner], out_ref.at[which, inner], sems.at[which, 0]))
        copies[-1].start()

    def stages(step):
        for which in range(views):
            for end in range(2):
                at = which * 2 + end
                yield (
                    (lambda j, which=which, end=end: edge_ref[which, end, j]) if step == 1 else (lambda j, at=at: work[at, j]),
                    functools.partial(put_tile, work, at),
                )

    scan_tiles(stages, None, blocks)
    for which in range(views):
        for end in range(2):
            first = end * (rows - SUB)
            peak = tall[which, first : first + SUB, :]
            for j in range(blocks):
                peak = jnp.maximum(peak, work[which * 2 + end, j])
                stage[which, first : first + SUB, j * LANE : (j + 1) * LANE] = peak - edge_ref[which, end, j]
            outer = pl.ds(first, SUB)
            copies.append(pltpu.make_async_copy(stage.at[which, outer], out_ref.at[which, outer], sems.at[which, 1 + end]))
            copies[-1].start()
    for copy in copies:
        copy.wait()


def on_device(ty, tx, surface, bearing, disp, altitude):
    rows, cols = surface.shape
    views = bearing.shape[0]
    tiles, blocks = rows // SUB, cols // LANE
    f32 = jnp.float32
    up = lax.ppermute(surface[rows - SUB :], "ty", [(i, (i + 1) % ty) for i in range(ty)])
    down = lax.ppermute(surface[:SUB], "ty", [((i + 1) % ty, i) for i in range(ty)])
    smem = pl.BlockSpec(memory_space=pltpu.SMEM)
    vmem = pl.BlockSpec(memory_space=pltpu.VMEM)
    hbm = pl.BlockSpec(memory_space=pl.ANY)
    lifted, margin, edge, peak = pl.pallas_call(
        functools.partial(inner_kernel, tx=tx),
        out_shape=(
            pltpu.VMEM((views, tiles, blocks, SUB, LANE), f32),
            pltpu.VMEM((views, tiles, blocks, SUB, LANE), f32),
            pltpu.VMEM((2, blocks, 2 * SUB, LANE), f32),
            pltpu.VMEM((views, tiles, SUB, LANE), f32),
        ),
        in_specs=[smem, smem, smem, hbm],
        out_specs=[vmem] * 4,
        scratch_shapes=[
            pltpu.VMEM((blocks, rows, LANE), f32),
            pltpu.VMEM((tiles, blocks, SUB, LANE), f32),
            pltpu.SemaphoreType.DMA((blocks,)),
        ],
        compiler_params=pltpu.CompilerParams(vmem_limit_bytes=24 * MIB),
        cost_estimate=pl.CostEstimate(flops=views * rows * cols * 40, bytes_accessed=rows * cols * 4, transcendentals=0),
        name="inner",
    )(bearing, disp, altitude, surface)
    outer, sent = pl.pallas_call(
        functools.partial(edge_kernel, tx=tx, ty=ty),
        out_shape=(
            pltpu.VMEM((views, 2, blocks, SUB, LANE), f32),
            jax.ShapeDtypeStruct((tx, views, rows), f32),
        ),
        in_specs=[smem, smem, smem] + [vmem] * 4,
        out_specs=[vmem] * 2,
        scratch_shapes=[pltpu.VMEM((2, blocks, 3 * SUB, LANE), f32), pltpu.VMEM((rows, LANE), f32)],
        compiler_params=pltpu.CompilerParams(vmem_limit_bytes=16 * MIB),
        name="edges",
    )(bearing, disp, altitude, up, down, edge, peak)
    got = lax.all_to_all(sent, "tx", 0, 0)
    return pl.pallas_call(
        functools.partial(final_kernel, tx=tx),
        out_shape=jax.ShapeDtypeStruct((views, rows, cols), f32),
        in_specs=[vmem] * 4,
        out_specs=hbm,
        scratch_shapes=[
            pltpu.VMEM((views, rows, cols), f32),
            pltpu.VMEM((views * 2, blocks, SUB, LANE), f32),
            pltpu.VMEM((views, rows, LANE), f32),
            pltpu.SemaphoreType.DMA((views, 3)),
        ],
        compiler_params=pltpu.CompilerParams(vmem_limit_bytes=24 * MIB),
        name="finish",
    )(got, lifted, margin, outer)


def solution(mesh):
    return jax.shard_map(
        functools.partial(on_device, mesh.shape["ty"], mesh.shape["tx"]),
        mesh=mesh,
        in_specs=(P("ty", "tx"), P(), P(), P()),
        out_specs=P(None, "ty", "tx"),
        check_vma=False,
    )
```

time: 89.5 us -> 32.3 us (0.36)
  the two profiles are of different devices: /device:TPU:13 before, /device:TPU:0 now
where the time goes in v1:
time: 32.3 us; the launch traced here: 32 us
  Pallas kernels  13.6 us (42%)
  blocking collectives  10.3 us (32%)
  local copies, waits for them, and re-layouts  4.07 us (13%)
  starting transfers between devices  3.98 us (12%)
    all_to_all x1, blocking collectives, on_device(): got = lax.all_to_all(sent, 'tx', 0, 0)  10.3 us
    pallas_call x1, Pallas kernels, on_device(): pl.pallas_call(functools.partial(inner_kernel, tx=tx), out_shape=(pltpu.V...  10.1 us
    ppermute x1, starting transfers between devices, on_device(): lax.ppermute(surface[:SUB], 'ty', [((i + 1) % ty, i) for i in range(ty)])  3.97 us
    unnamed x8, local copies, waits for them, and re-layouts  3.19 us
    pallas_call x1, Pallas kernels, on_device(): pl.pallas_call(functools.partial(final_kernel, tx=tx), out_shape=jax.Shap...  2.57 us
    pallas_call x1, Pallas kernels, on_device(): pl.pallas_call(functools.partial(edge_kernel, tx=tx, ty=ty), out_shape=(p...  0.91 us
    slice x1, local copies, waits for them, and re-layouts, on_device(): surface[:SUB]  0.88 us
  transfers between devices with their start and end apart: 2, of which 0 were waited for; matrix products, arithmetic and copies ran while one was open for 0% of the time, Pallas kernels for 32%

profile of v1, /device:TPU:0, one launch (start us, length us, event | category | flops | bytes accessed | tf_op | source)
XLA Modules:
  0.0 32.0 jit_solution(8829008118969641234)
XLA Ops:
  0.0 0.9 %fusion = (f32[8,2048]{1,0:T(8,128)S(1)}, f32[8,2048]{1,0:T(8,128)S(1)}) fusion(f32[128,2048]{1,0:T(8,128)} %x_ref.1), kind=kLoop, calls=%fused_computation | loop fusion | bytes 262144 | tf_op jit(solution)/shard_map/slice | solution.py:200
  0.9 4.0 %collective-permute-start.1 = (f32[8,2048]{1,0:T(8,128)S(1)}, f32[8,2048]{1,0:T(8,128)S(1)}, u32[]{:S(2)}, u32[]{:S(2)}) collective-permute-start(f32[8,2048]{1,0:T(8,128)S(1)} %get-tuple-element.17), channel_id=1, source_target_pairs={{8,0},{16,8},{24,16},{0,24},{9,1},{17,9},{25,17},{1,25},{10,2},{18... | collective-permute-start | bytes 196616 | tf_op jit(solution)/shard_map/ppermute | solution.py:200
  4.9 0.0 collective-permute-start
  4.9 0.0 copy-start
  4.9 1.2 %copy-done = f32[128,2048]{1,0:T(8,128)S(1)} copy-done((f32[128,2048]{1,0:T(8,128)S(1)}, f32[128,2048]{1,0:T(8,128)}, u32[]{:S(2)}) %copy-start) | copy-done | bytes 1048600
  6.1 0.0 copy-start.1
  6.1 0.7 %copy-done.1 = s32[4]{0:T(128)S(1)} copy-done((s32[4]{0:T(128)S(1)}, s32[4]{0:T(128)}, u32[]{:S(2)}) %copy-start.1) | copy-done | bytes 40
  6.7 0.0 copy-start.2
  6.7 0.7 %copy-done.2 = s32[4]{0:T(128)S(1)} copy-done((s32[4]{0:T(128)S(1)}, s32[4]{0:T(128)}, u32[]{:S(2)}) %copy-start.2) | copy-done | bytes 40
  7.4 0.0 copy-start.3
  7.4 0.7 %copy-done.3 = s32[4]{0:T(128)S(1)} copy-done((s32[4]{0:T(128)S(1)}, s32[4]{0:T(128)}, u32[]{:S(2)}) %copy-start.3) | copy-done | bytes 40
  8.1 10.1 %inner.1 = (f32[4,16,16,8,128]{4,3,2,1,0:T(8,128)S(1)}, f32[4,16,16,8,128]{4,3,2,1,0:T(8,128)S(1)}, f32[2,16,16,128]{3,2,1,0:T(8,128)S(1)}, f32[4,16,8,128]{3,2,1,0:T(8,128)S(1)}) custom-call(s32[4]{0:T(128)S(1)} %copy-done.1, s32[4]{0:T(128)S(1)} %copy-done.2, s32[4]{0:T(128)S(1)} %copy-done.3, f32[128,2048]{1,0:T(8,128)S(1)} %copy-done), custom_call_target="tpu_custom_call" | custom-call | flops 41943040 | bytes 1048576 | tf_op jit(solution)/shard_map/inner/pallas_call | solution.py:204
  18.2 0.0 collective-permute-done.1.down_ref
  18.2 0.0 collective-permute-done.up_ref
  18.2 0.9 %edges.1 = (f32[4,2,16,8,128]{4,3,2,1,0:T(8,128)S(1)}, f32[8,4,128]{2,1,0:T(4,128)S(1)}) custom-call(s32[4]{0:T(128)S(1)} %copy-done.1, s32[4]{0:T(128)S(1)} %copy-done.2, s32[4]{0:T(128)S(1)} %copy-done.3, f32[8,2048]{1,0:T(8,128)S(1)} %collective-permute-done.up_ref, f32[8,2048]{1,0:T(8,128)S(1)} %collective-permute-done.1.down_ref, ...), custom_call_target="tpu_custom_call" | custom-call | tf_op jit(solution)/shard_map/edges/pallas_call | solution.py:223
  19.1 10.3 %all_to_all.5.got_ref = f32[8,4,128]{2,1,0:T(4,128)S(1)} all-to-all(f32[8,4,128]{2,1,0:T(4,128)S(1)} %get-tuple-element.13), channel_id=1, replica_groups=mesh['ty'=4,'tx'=8] {'tx'}, dimensions={0} | all-to-all | bytes 32768 | tf_op jit(solution)/shard_map/all_to_all | solution.py:235
  29.5 2.6 %finish.1 = f32[4,128,2048]{2,1,0:T(8,128)} custom-call(f32[8,4,128]{2,1,0:T(4,128)S(1)} %all_to_all.5.got_ref, f32[4,16,16,8,128]{4,3,2,1,0:T(8,128)S(1)} %get-tuple-element.14.lifted_ref, f32[4,16,16,8,128]{4,3,2,1,0:T(8,128)S(1)} %get-tuple-element.15.margin_ref, f32[4,2,16,8,128]{4,3,2,1,0:T(8,128)S(1)} %get-tuple-element.16.edge_ref), custom_call_target="tpu_custom_call" | custom-call | tf_op jit(solution)/shard_map/finish/pallas_call | solution.py:236
Async XLA Ops:
  0.9 17.3 %collective-permute-start.1 = (f32[8,2048]{1,0:T(8,128)S(1)}, f32[8,2048]{1,0:T(8,128)S(1)}, u32[]{:S(2)}, u32[]{:S(2)}) collective-permute-start(f32[8,2048]{1,0:T(8,128)S(1)} %get-tuple-element.17), channel_id=1, source_target_pairs={{8,0},{16,8},{24,16},{0,24},{9,1},{17,9},{25,17},{1,25},{10,2},{18... | collective-permute-start | bytes 196616 | tf_op jit(solution)/shard_map/ppermute | solution.py:200
  4.9 13.4 %collective-permute-start = (f32[8,2048]{1,0:T(8,128)S(1)}, f32[8,2048]{1,0:T(8,128)S(1)}, u32[]{:S(2)}, u32[]{:S(2)}) collective-permute-start(f32[8,2048]{1,0:T(8,128)S(1)} %get-tuple-element.18), channel_id=1, source_target_pairs={{0,8},{8,16},{16,24},{24,0},{1,9},{9,17},{17,25},{25,1},{2,10},{10... | collective-permute-start | bytes 196616 | tf_op jit(solution)/shard_map/ppermute | solution.py:199
  4.9 1.2 %copy-start = (f32[128,2048]{1,0:T(8,128)S(1)}, f32[128,2048]{1,0:T(8,128)}, u32[]{:S(2)}) copy-start(f32[128,2048]{1,0:T(8,128)} %x_ref.1) | copy-start | bytes 3145732
  6.1 0.7 %copy-start.1 = (s32[4]{0:T(128)S(1)}, s32[4]{0:T(128)}, u32[]{:S(2)}) copy-start(s32[4]{0:T(128)} %bearing_ref.3) | copy-start | bytes 52
  6.7 0.7 %copy-start.2 = (s32[4]{0:T(128)S(1)}, s32[4]{0:T(128)}, u32[]{:S(2)}) copy-start(s32[4]{0:T(128)} %disp_ref.3) | copy-start | bytes 52
  7.4 0.7 %copy-start.3 = (s32[4]{0:T(128)S(1)}, s32[4]{0:T(128)}, u32[]{:S(2)}) copy-start(s32[4]{0:T(128)} %class_ref.3) | copy-start | bytes 52

commit v2 on v1

v2 whole, which is shorter than its diff:
```python
import functools
import math

import jax
import jax.numpy as jnp
from jax import lax
from jax.experimental import pallas as pl
from jax.experimental.pallas import tpu as pltpu
from jax.sharding import PartitionSpec as P

TAPS = 4
SUB = 8
LANE = 128
MIB = 1 << 20
EARLY = 1


def view_terms(bearing_ref, class_ref, which, easting_span):
    bearing = bearing_ref[which]
    frac = (lax.rem(bearing * 5, 16).astype(jnp.float32) + 0.5) * 0.0625
    theta = (bearing.astype(jnp.float32) - 7.5) * (math.pi / 32.0)
    stride = 1.0 / jnp.cos(jnp.full((SUB, LANE), theta, jnp.float32))
    slope = (1.0 + class_ref[which].astype(jnp.float32)) * (1.0 / (4.0 * easting_span))
    cube = frac * frac * frac
    square = frac * frac
    weights = (
        (-cube + 2.0 * square - frac) * 0.5,
        (3.0 * cube - 5.0 * square + 2.0) * 0.5,
        (-3.0 * cube + 4.0 * square + frac) * 0.5,
        (cube - square) * 0.5,
    )
    return weights, stride * slope


def column_tile(first_col, block):
    lane = lax.broadcasted_iota(jnp.int32, (SUB, LANE), 1)
    return (lane + (first_col + block * LANE)).astype(jnp.float32)


def lifted_tile(weights, ramp, rows_at):
    total = weights[0] * rows_at(0)
    for tap in range(1, TAPS):
        total = total + weights[tap] * rows_at(tap)
    return total + ramp


def scan_tiles(count, load, work, blocks):
    lane = lax.broadcasted_iota(jnp.int32, (SUB, LANE), 1)
    lowest = jnp.full((SUB, LANE), -jnp.inf, jnp.float32)
    step = 1
    while step < LANE:
        for t in range(count):
            values = [load(t, j) if step == 1 else work[t, j] for j in range(blocks)]
            left = lowest
            for j in range(blocks):
                here = pltpu.roll(values[j], step, 1)
                work[t, j] = jnp.maximum(values[j], jnp.where(lane < step, left, here))
                left = here
        step *= 2


def scan_view(count, load, store, work, blocks):
    scan_tiles(count, load, work, blocks)
    for t in range(count):
        peak = work[t, 0]
        store(t, 0, peak - load(t, 0))
        for j in range(1, blocks):
            peak = jnp.maximum(peak, work[t, j])
            store(t, j, peak - load(t, j))


def inner_kernel(
    bearing_hbm, disp_hbm, class_hbm, x_ref, lifted_ref, margin_ref, edge_ref, peak_ref, terms_ref, disp_out,
    own, work, bearing_ref, disp_ref, class_ref, sems, few_sems, *, tx,
):
    rows, cols = x_ref.shape
    blocks, tiles = cols // LANE, rows // SUB
    views = bearing_ref.shape[0]
    few = [
        pltpu.make_async_copy(source, target, few_sems.at[i])
        for i, (source, target) in enumerate(((bearing_hbm, bearing_ref), (disp_hbm, disp_ref), (class_hbm, class_ref)))
    ]
    for copy in few:
        copy.start()
    copies = [
        pltpu.make_async_copy(x_ref.at[:, pl.ds(j * LANE, LANE)], own.at[j], sems.at[j])
        for j in range(blocks)
    ]
    for copy in copies:
        copy.start()
    first_col = lax.axis_index("tx") * cols
    for copy in few:
        copy.wait()
    for which in range(views):
        weights, rise = view_terms(bearing_ref, class_ref, which, cols * tx)
        disp_out[which] = disp_ref[which]
        for tap in range(TAPS):
            terms_ref[which, tap] = jnp.full((SUB, LANE), weights[tap], jnp.float32)
        terms_ref[which, TAPS] = rise
        for t in range(1, tiles - 1):
            peak_ref[which, t] = jnp.full((SUB, LANE), -jnp.inf, jnp.float32)

    for copy in copies:
        copy.wait()

    @pl.loop(0, blocks)
    def _(j):
        edge_ref[0, j] = own[j, 0 : 2 * SUB, :]
        edge_ref[1, j] = own[j, rows - 2 * SUB : rows, :]
        column = column_tile(first_col, j)
        for which in range(views):
            weights = [terms_ref[which, tap] for tap in range(TAPS)]
            ramp = terms_ref[which, TAPS] * column
            disp = disp_ref[which] - 1
            for t in range(1, tiles - 1):
                value = lifted_tile(weights, ramp, lambda tap: own[j, pl.ds(t * SUB + disp + tap, SUB), :])
                lifted_ref[which, t, j] = value
                peak_ref[which, t] = jnp.maximum(peak_ref[which, t], value)

    for which in range(EARLY):
        scan_view(
            tiles - 2,
            lambda t, j: lifted_ref[which, t + 1, j],
            functools.partial(put_tile, margin_ref, which),
            work,
            blocks,
        )


def put_tile(ref, which, t, j, value):
    ref[which, t, j] = value


def edge_kernel(disp_ref, terms_ref, up_ref, down_ref, edge_ref, peak_ref, lifted_ref, sent_ref, ring, tall, *, ty):
    cols = up_ref.shape[1]
    blocks = cols // LANE
    views, tiles = peak_ref.shape[:2]
    place = lax.axis_index("ty")
    first_col = lax.axis_index("tx") * cols
    for j in range(blocks):
        span = slice(j * LANE, (j + 1) * LANE)
        ring[0, j, 0:SUB, :] = jnp.where(place == 0, 0.0, up_ref[:, span])
        ring[0, j, SUB : 3 * SUB, :] = edge_ref[0, j]
        ring[1, j, 0 : 2 * SUB, :] = edge_ref[1, j]
        ring[1, j, 2 * SUB : 3 * SUB, :] = jnp.where(place == ty - 1, 0.0, down_ref[:, span])
    for which in range(views):
        weights, rise = [terms_ref[which, tap] for tap in range(TAPS)], terms_ref[which, TAPS]
        disp = disp_ref[which] - 1
        tops = []
        for end in range(2):
            top = None
            for j in range(blocks):
                value = lifted_tile(
                    weights,
                    rise * column_tile(first_col, j),
                    lambda tap: ring[end, j, pl.ds(SUB + disp + tap, SUB), :],
                )
                lifted_ref[which, end, j] = value
                top = value if top is None else jnp.maximum(top, value)
            tops.append(top)
        tall[0:SUB, :] = tops[0]
        for t in range(1, tiles - 1):
            tall[t * SUB : (t + 1) * SUB, :] = peak_ref[which, t]
        tall[(tiles - 1) * SUB : tiles * SUB, :] = tops[1]
        sent_ref[which : which + 1, :] = jnp.max(jnp.transpose(tall[...]), axis=0, keepdims=True)


def late_kernel(lifted_ref, edge_ref, margin_ref, edge_margin_ref, work):
    views, tiles, blocks = lifted_ref.shape[:3]

    @pl.loop(EARLY, views)
    def _(which):
        scan_view(
            tiles - 2,
            lambda t, j: lifted_ref[which, t + 1, j],
            functools.partial(put_tile, margin_ref, which - EARLY),
            work,
            blocks,
        )

    scan_view(
        views * 2,
        lambda t, j: edge_ref[t // 2, t % 2, j],
        lambda t, j, value: put_tile(edge_margin_ref, t // 2, t % 2, j, value),
        work,
        blocks,
    )


def final_kernel(*refs, tx):
    partner_ref, *got_refs = refs[: tx // 2]
    lifted_ref, early_ref, late_ref, edge_ref, edge_margin_ref, out_ref, stage, tall, sems = refs[tx // 2 :]
    views, rows, cols = out_ref.shape
    blocks, tiles = cols // LANE, rows // SUB
    place = lax.axis_index("tx")
    chip = place // 2
    before = jnp.where(lax.rem(place, 2) == 1, partner_ref[...], -jnp.inf)
    for i, got_ref in enumerate(got_refs):
        before = jnp.maximum(before, jnp.where((chip ^ (i + 1)) < chip, got_ref[...], -jnp.inf))
    for which in range(views):
        tall[which] = jnp.transpose(jnp.broadcast_to(before[which : which + 1, :], (LANE, rows)))
    copies = []
    for which in range(views):
        margin = early_ref.at[which] if which < EARLY else late_ref.at[which - EARLY]

        def put(t, margin_at, lifted_at):
            span = pl.ds(t * SUB, SUB)
            top = tall[which, span, :]
            for j in range(blocks):
                stage[which, span, j * LANE : (j + 1) * LANE] = jnp.maximum(margin_at(j), top - lifted_at(j))

        for end in range(2):
            put(
                end * (tiles - 1),
                lambda j: edge_margin_ref[which, end, j],
                lambda j: edge_ref[which, end, j],
            )

        @pl.loop(1, tiles - 1)
        def _(t):
            put(t, lambda j: margin[t - 1, j], lambda j: lifted_ref[which, t, j])

        copies.append(pltpu.make_async_copy(stage.at[which], out_ref.at[which], sems.at[which]))
        copies[-1].start()
    for copy in copies:
        copy.wait()


def on_device(ty, tx, surface, bearing, disp, altitude):
    rows, cols = surface.shape
    views = bearing.shape[0]
    tiles, blocks = rows // SUB, cols // LANE
    f32 = jnp.float32
    assert tx & (tx - 1) == 0 and tx > 1
    up = lax.ppermute(surface[rows - SUB :], "ty", [(i, (i + 1) % ty) for i in range(ty)])
    down = lax.ppermute(surface[:SUB], "ty", [((i + 1) % ty, i) for i in range(ty)])
    smem = pl.BlockSpec(memory_space=pltpu.SMEM)
    vmem = pl.BlockSpec(memory_space=pltpu.VMEM)
    hbm = pl.BlockSpec(memory_space=pltpu.HBM)
    tile = (SUB, LANE)
    pinned = [pltpu.with_memory_space_constraint(a, pltpu.HBM) for a in (bearing, disp, altitude, surface)]
    lifted, early, edge, peak, terms, shifts = pl.pallas_call(
        functools.partial(inner_kernel, tx=tx),
        out_shape=(
            pltpu.VMEM((views, tiles, blocks) + tile, f32),
            pltpu.VMEM((EARLY, tiles - 2, blocks) + tile, f32),
            pltpu.VMEM((2, blocks, 2 * SUB, LANE), f32),
            pltpu.VMEM((views, tiles) + tile, f32),
            pltpu.VMEM((views, TAPS + 1) + tile, f32),
            pltpu.SMEM((views,), jnp.int32),
        ),
        in_specs=[hbm] * 4,
        out_specs=[vmem] * 5 + [smem],
        scratch_shapes=[
            pltpu.VMEM((blocks, rows, LANE), f32),
            pltpu.VMEM((tiles - 2, blocks) + tile, f32),
            pltpu.SMEM((views,), jnp.int32),
            pltpu.SMEM((views,), jnp.int32),
            pltpu.SMEM((views,), jnp.int32),
            pltpu.SemaphoreType.DMA((blocks,)),
            pltpu.SemaphoreType.DMA((3,)),
        ],
        compiler_params=pltpu.CompilerParams(vmem_limit_bytes=16 * MIB),
        cost_estimate=pl.CostEstimate(flops=views * rows * cols * 40, bytes_accessed=rows * cols * 4, transcendentals=0),
        name="inner",
    )(*pinned)
    outer, peaks = pl.pallas_call(
        functools.partial(edge_kernel, ty=ty),
        out_shape=(pltpu.VMEM((views, 2, blocks) + tile, f32), pltpu.VMEM((views, rows), f32)),
        in_specs=[smem] + [vmem] * 5,
        out_specs=[vmem] * 2,
        scratch_shapes=[pltpu.VMEM((2, blocks, 3 * SUB, LANE), f32), pltpu.VMEM((rows, LANE), f32)],
        compiler_params=pltpu.CompilerParams(vmem_limit_bytes=16 * MIB),
        name="edges",
    )(shifts, terms, up, down, edge, peak)
    partner = lax.ppermute(peaks, "tx", [(i, i ^ 1) for i in range(tx)])
    chip_peaks = jnp.maximum(peaks, partner)
    got = [lax.ppermute(chip_peaks, "tx", [(i, i ^ m) for i in range(tx)]) for m in range(2, tx, 2)]
    late, outer_margin = pl.pallas_call(
        late_kernel,
        out_shape=(
            pltpu.VMEM((views - EARLY, tiles - 2, blocks) + tile, f32),
            pltpu.VMEM((views, 2, blocks) + tile, f32),
        ),
        in_specs=[vmem] * 2,
        out_specs=[vmem] * 2,
        scratch_shapes=[pltpu.VMEM((max(tiles - 2, 2 * views), blocks) + tile, f32)],
        compiler_params=pltpu.CompilerParams(vmem_limit_bytes=16 * MIB),
        cost_estimate=pl.CostEstimate(flops=views * rows * cols * 40, bytes_accessed=rows * cols * 4, transcendentals=0),
        name="late",
    )(lifted, outer)
    return pl.pallas_call(
        functools.partial(final_kernel, tx=tx),
        out_shape=jax.ShapeDtypeStruct((views, rows, cols), f32),
        in_specs=[vmem] * (tx // 2 + 5),
        out_specs=hbm,
        scratch_shapes=[
            pltpu.VMEM((views, rows, cols), f32),
            pltpu.VMEM((views, rows, LANE), f32),
            pltpu.SemaphoreType.DMA((views,)),
        ],
        compiler_params=pltpu.CompilerParams(vmem_limit_bytes=16 * MIB),
        name="finish",
    )(partner, *got, lifted, early, late, outer, outer_margin)


def solution(mesh):
    return jax.shard_map(
        functools.partial(on_device, mesh.shape["ty"], mesh.shape["tx"]),
        mesh=mesh,
        in_specs=(P("ty", "tx"), P(), P(), P()),
        out_specs=P(None, "ty", "tx"),
        check_vma=False,
    )
```

time: 32.3 us -> 24.7 us (0.76)
  blocking collectives: 10.3 us -> 0 us
  starting transfers between devices: 3.98 us -> 8.44 us
  local copies, waits for them, and re-layouts: 4.07 us -> 0.88 us
  waiting for transfers between devices: 0.01 us -> 1.74 us
    all_to_all x1 -> x0, blocking collectives: 10.3 us -> none  [on_device(): got = lax.all_to_all(sent, 'tx', 0, 0)]
    pallas_call x1, Pallas kernels: 10.1 us -> 4.57 us  [on_device(): pl.pallas_call(functools.partial(inner_kernel, tx=tx), out_shape=(pltpu.V...]
    pallas_call x1 -> x2, Pallas kernels: 0.91 us -> 6.45 us  [the longest x1 6.16 us: on_device(): pl.pallas_call(late_kernel, out_shape=(pltpu.VMEM((views - EARLY, tiles -...]
    ppermute x0 -> x4, starting transfers between devices: none -> 4.46 us  [the longest x3 4.39 us: on_device(): lax.ppermute(chip_peaks, 'tx', [(i, i ^ m) for i in range(tx)])]
    unnamed x8 -> x0, local copies, waits for them, and re-layouts: 3.19 us -> none
    ppermute x0 -> x4, waiting for transfers between devices: none -> 1.16 us  [the longest x1 1.15 us: on_device(): partner = lax.ppermute(peaks, 'tx', [(i, i ^ 1) for i in range(tx)])]
    ppermute x1, waiting for transfers between devices: 0.01 us -> 0.58 us  [on_device(): lax.ppermute(surface[rows - SUB:], 'ty', [(i, (i + 1) % ty) for i in rang...]
  transfers between devices with their start and end apart: 2 -> 6, of which waited for: 0 -> 2; matrix products, arithmetic and copies ran while one was open for 0% -> 0% of each run, Pallas kernels for 32% -> 44%
where the time goes in v2:
time: 24.7 us; the launch traced here: 24.5 us
  Pallas kernels  13.4 us (54%)
  starting transfers between devices  8.44 us (34%)
  waiting for transfers between devices  1.74 us (7%)
  local copies, waits for them, and re-layouts  0.88 us (4%)
    pallas_call x1, Pallas kernels, on_device(): pl.pallas_call(late_kernel, out_shape=(pltpu.VMEM((views - EARLY, tiles -...  6.16 us
    pallas_call x1, Pallas kernels, on_device(): pl.pallas_call(functools.partial(inner_kernel, tx=tx), out_shape=(pltpu.V...  4.57 us
    ppermute x3, starting transfers between devices, on_device(): lax.ppermute(chip_peaks, 'tx', [(i, i ^ m) for i in range(tx)])  4.39 us
    ppermute x1, starting transfers between devices, on_device(): lax.ppermute(surface[:SUB], 'ty', [((i + 1) % ty, i) for i in range(ty)])  3.97 us
    pallas_call x1, Pallas kernels, on_device(): pl.pallas_call(functools.partial(final_kernel, tx=tx), out_shape=jax.Shap...  2.35 us
    ppermute x1, waiting for transfers between devices, on_device(): partner = lax.ppermute(peaks, 'tx', [(i, i ^ 1) for i in range(tx)])  1.15 us
    slice x1, local copies, waits for them, and re-layouts, on_device(): surface[:SUB]  0.88 us
    ppermute x1, waiting for transfers between devices, on_device(): lax.ppermute(surface[rows - SUB:], 'ty', [(i, (i + 1) % ty) for i in rang...  0.58 us
  transfers between devices with their start and end apart: 6, of which 2 were waited for; matrix products, arithmetic and copies ran while one was open for 0% of the time, Pallas kernels for 44%

profile of v2, /device:TPU:0, one launch (start us, length us, event | category | flops | bytes accessed | tf_op | source)
XLA Modules:
  0.0 24.5 jit_solution(1344170962937552326)
XLA Ops:
  0.0 0.9 %fusion = (f32[8,2048]{1,0:T(8,128)S(1)}, f32[8,2048]{1,0:T(8,128)S(1)}) fusion(f32[128,2048]{1,0:T(8,128)} %x_ref.1), kind=kLoop, calls=%fused_computation | loop fusion | bytes 262144 | tf_op jit(solution)/shard_map/slice | solution.py:236
  0.9 4.0 %collective-permute-start.1 = (f32[8,2048]{1,0:T(8,128)S(1)}, f32[8,2048]{1,0:T(8,128)S(1)}, u32[]{:S(2)}, u32[]{:S(2)}) collective-permute-start(f32[8,2048]{1,0:T(8,128)S(1)} %get-tuple-element.25), channel_id=1, source_target_pairs={{8,0},{16,8},{24,16},{0,24},{9,1},{17,9},{25,17},{1,25},{10,2},{18... | collective-permute-start | bytes 196616 | tf_op jit(solution)/shard_map/ppermute | solution.py:236
  4.9 0.0 collective-permute-start
  4.9 4.6 %inner.1 = (f32[4,16,16,8,128]{4,3,2,1,0:T(8,128)S(1)}, f32[1,14,16,8,128]{4,3,2,1,0:T(8,128)S(1)}, f32[2,16,16,128]{3,2,1,0:T(8,128)S(1)}, f32[4,16,8,128]{3,2,...) custom-call(s32[4]{0:T(128)} %bearing_hbm.1, s32[4]{0:T(128)} %disp_hbm.1, s32[4]{0:T(128)} %class_hbm.1, ...), custom_call_target="tpu_custom_call" | custom-call | flops 41943040 | bytes 1048576 | tf_op jit(solution)/shard_map/inner/pallas_call | solution.py:242
  9.4 0.0 collective-permute-done.1.down_ref
  9.4 0.6 %collective-permute-done.up_ref = f32[8,2048]{1,0:T(8,128)S(1)} collective-permute-done((f32[8,2048]{1,0:T(8,128)S(1)}, f32[8,2048]{1,0:T(8,128)S(1)}, u32[]{:S(2)}, u32[]{:S(2)}) %collective-permute-start) | collective-permute-done | bytes 65568 | tf_op jit(solution)/shard_map/ppermute | solution.py:235
  10.0 0.3 %edges.1 = (f32[4,2,16,8,128]{4,3,2,1,0:T(8,128)S(1)}, f32[4,128]{1,0:T(4,128)S(1)}) custom-call(s32[4]{0:T(128)S(4)} %get-tuple-element.15.disp_ref, f32[4,5,8,128]{3,2,1,0:T(8,128)S(1)} %get-tuple-element.16.terms_ref, f32[8,2048]{1,0:T(8,128)S(1)} %collective-permute-done.up_ref, f32[8,2048]{1,0:T(8,128)S(1)} %collective-permute-done.1.down_ref, ...), custom_call_target="tpu_custom_call" | custom-call | tf_op jit(solution)/shard_map/edges/pallas_call | solution.py:267
  10.3 0.1 collective-permute-start.2
  10.4 1.1 %collective-permute-done.2.refs_0_ = f32[4,128]{1,0:T(4,128)S(1)} collective-permute-done((f32[4,128]{1,0:T(4,128)S(1)}, f32[4,128]{1,0:T(4,128)S(1)}, u32[]{:S(2)}, u32[]{:S(2)}) %collective-permute-start.2) | collective-permute-done | bytes 2080 | tf_op jit(solution)/shard_map/ppermute | solution.py:276
  11.5 3.6 %collective-permute-start.5 = (f32[4,128]{1,0:T(4,128)S(1)}, f32[4,128]{1,0:T(4,128)S(1)}, u32[]{:S(2)}, u32[]{:S(2)}) collective-permute-start(f32[4,128]{1,0:T(4,128)S(1)} %max.3), channel_id=1, source_target_pairs={{0,6},{1,7},{2,4},{3,5},{4,2},{5,3},{6,0},{7,1},{8,14},{9,15},{10,... | collective-permute-start | bytes 6152 | tf_op jit(solution)/shard_map/ppermute | solution.py:278
  15.1 0.0 collective-permute-start.4
  15.1 0.8 %collective-permute-start.3 = (f32[4,128]{1,0:T(4,128)S(1)}, f32[4,128]{1,0:T(4,128)S(1)}, u32[]{:S(2)}, u32[]{:S(2)}) collective-permute-start(f32[4,128]{1,0:T(4,128)S(1)} %max.3), channel_id=1, source_target_pairs={{0,2},{1,3},{2,0},{3,1},{4,6},{5,7},{6,4},{7,5},{8,10},{9,11},{10,... | collective-permute-start | bytes 6152 | tf_op jit(solution)/shard_map/ppermute | solution.py:278
  15.9 6.2 %late.1 = (f32[3,14,16,8,128]{4,3,2,1,0:T(8,128)S(1)}, f32[4,2,16,8,128]{4,3,2,1,0:T(8,128)S(1)}) custom-call(f32[4,16,16,8,128]{4,3,2,1,0:T(8,128)S(1)} %get-tuple-element.20.lifted_ref.refs_4_, f32[4,2,16,8,128]{4,3,2,1,0:T(8,128)S(1)} %get-tuple-element.22.edge_ref.refs_7_), custom_call_target="tpu_custom_call" | custom-call | flops 41943040 | bytes 1048576 | tf_op jit(solution)/shard_map/late/pallas_call | solution.py:279
  22.1 0.0 collective-permute-done.5.refs_3_
  22.1 0.0 collective-permute-done.4.refs_2_
  22.1 0.0 collective-permute-done.3.refs_1_
  22.1 2.4 %finish.1 = f32[4,128,2048]{2,1,0:T(8,128)} custom-call(f32[4,128]{1,0:T(4,128)S(1)} %collective-permute-done.2.refs_0_, f32[4,128]{1,0:T(4,128)S(1)} %collective-permute-done.3.refs_1_, f32[4,128]{1,0:T(4,128)S(1)} %collective-permute-done.4.refs_2_, f32[4,128]{1,0:T(4,128)S(1)} %collective-permute-done.5.refs_3_, ...), custom_call_target="tpu_custom_call" | custom-call | tf_op jit(solution)/shard_map/finish/pallas_call | solution.py:292
  (1 shorter events, 0.0 us)
Async XLA Ops:
  0.9 8.6 %collective-permute-start.1 = (f32[8,2048]{1,0:T(8,128)S(1)}, f32[8,2048]{1,0:T(8,128)S(1)}, u32[]{:S(2)}, u32[]{:S(2)}) collective-permute-start(f32[8,2048]{1,0:T(8,128)S(1)} %get-tuple-element.25), channel_id=1, source_target_pairs={{8,0},{16,8},{24,16},{0,24},{9,1},{17,9},{25,17},{1,25},{10,2},{18... | collective-permute-start | bytes 196616 | tf_op jit(solution)/shard_map/ppermute | solution.py:236
  4.9 5.2 %collective-permute-start = (f32[8,2048]{1,0:T(8,128)S(1)}, f32[8,2048]{1,0:T(8,128)S(1)}, u32[]{:S(2)}, u32[]{:S(2)}) collective-permute-start(f32[8,2048]{1,0:T(8,128)S(1)} %get-tuple-element.26), channel_id=1, source_target_pairs={{0,8},{8,16},{16,24},{24,0},{1,9},{9,17},{17,25},{25,1},{2,10},{10... | collective-permute-start | bytes 196616 | tf_op jit(solution)/shard_map/ppermute | solution.py:235
  10.3 1.2 %collective-permute-start.2 = (f32[4,128]{1,0:T(4,128)S(1)}, f32[4,128]{1,0:T(4,128)S(1)}, u32[]{:S(2)}, u32[]{:S(2)}) collective-permute-start(f32[4,128]{1,0:T(4,128)S(1)} %get-tuple-element.19), channel_id=1, source_target_pairs={{0,1},{1,0},{2,3},{3,2},{4,5},{5,4},{6,7},{7,6},{8,9},{9,8},{10,11... | collective-permute-start | bytes 6152 | tf_op jit(solution)/shard_map/ppermute | solution.py:276
  11.5 10.6 %collective-permute-start.5 = (f32[4,128]{1,0:T(4,128)S(1)}, f32[4,128]{1,0:T(4,128)S(1)}, u32[]{:S(2)}, u32[]{:S(2)}) collective-permute-start(f32[4,128]{1,0:T(4,128)S(1)} %max.3), channel_id=1, source_target_pairs={{0,6},{1,7},{2,4},{3,5},{4,2},{5,3},{6,0},{7,1},{8,14},{9,15},{10,... | collective-permute-start | bytes 6152 | tf_op jit(solution)/shard_map/ppermute | solution.py:278
  15.1 7.0 %collective-permute-start.4 = (f32[4,128]{1,0:T(4,128)S(1)}, f32[4,128]{1,0:T(4,128)S(1)}, u32[]{:S(2)}, u32[]{:S(2)}) collective-permute-start(f32[4,128]{1,0:T(4,128)S(1)} %max.3), channel_id=1, source_target_pairs={{0,4},{1,5},{2,6},{3,7},{4,0},{5,1},{6,2},{7,3},{8,12},{9,13},{10,... | collective-permute-start | bytes 6152 | tf_op jit(solution)/shard_map/ppermute | solution.py:278
  15.1 7.0 %collective-permute-start.3 = (f32[4,128]{1,0:T(4,128)S(1)}, f32[4,128]{1,0:T(4,128)S(1)}, u32[]{:S(2)}, u32[]{:S(2)}) collective-permute-start(f32[4,128]{1,0:T(4,128)S(1)} %max.3), channel_id=1, source_target_pairs={{0,2},{1,3},{2,0},{3,1},{4,6},{5,7},{6,4},{7,5},{8,10},{9,11},{10,... | collective-permute-start | bytes 6152 | tf_op jit(solution)/shard_map/ppermute | solution.py:278

commit v3 on v2

v3 whole, which is shorter than its diff:
```python
import functools
import math

import jax
import jax.numpy as jnp
from jax import lax
from jax.experimental import pallas as pl
from jax.experimental.pallas import tpu as pltpu
from jax.sharding import PartitionSpec as P

TAPS = 4
SUB = 8
LANE = 128
MIB = 1 << 20
DELAY = 2


def view_terms(bearing_ref, class_ref, which, easting_span):
    bearing = bearing_ref[which]
    frac = (lax.rem(bearing * 5, 16).astype(jnp.float32) + 0.5) * 0.0625
    theta = (bearing.astype(jnp.float32) - 7.5) * (math.pi / 32.0)
    stride = 1.0 / jnp.cos(jnp.full((SUB, LANE), theta, jnp.float32))
    slope = (1.0 + class_ref[which].astype(jnp.float32)) * (1.0 / (4.0 * easting_span))
    cube = frac * frac * frac
    square = frac * frac
    weights = (
        (-cube + 2.0 * square - frac) * 0.5,
        (3.0 * cube - 5.0 * square + 2.0) * 0.5,
        (-3.0 * cube + 4.0 * square + frac) * 0.5,
        (cube - square) * 0.5,
    )
    return weights, stride * slope


def column_tile(first_col, block):
    lane = lax.broadcasted_iota(jnp.int32, (SUB, LANE), 1)
    return (lane + (first_col + block * LANE)).astype(jnp.float32)


def lifted_tile(weights, ramp, rows_at):
    total = weights[0] * rows_at(0)
    for tap in range(1, TAPS):
        total = total + weights[tap] * rows_at(tap)
    return total + ramp


def windows(tiles, carried):
    sub = lax.broadcasted_iota(jnp.int32, tiles[0].shape, 0)
    step = 1
    while step < SUB:
        here = [pltpu.roll(tile, step, 0) for tile in tiles]
        left = [carried[step]] + here[:-1]
        carried[step] = here[-1]
        tiles = [jnp.maximum(v, jnp.where(sub < step, p, q)) for v, p, q in zip(tiles, left, here)]
        step *= 2
    return tiles


def inner_kernel(
    bearing_hbm, disp_hbm, class_hbm, x_ref, lifted_ref, edge_ref, peak_ref, terms_ref, disp_out,
    own, bearing_ref, disp_ref, class_ref, sems, few_sems, *, tx,
):
    rows, cols = x_ref.shape
    blocks, tiles = cols // LANE, rows // SUB
    views = bearing_ref.shape[0]
    few = [
        pltpu.make_async_copy(source, target, few_sems.at[i])
        for i, (source, target) in enumerate(((bearing_hbm, bearing_ref), (disp_hbm, disp_ref), (class_hbm, class_ref)))
    ]
    for copy in few:
        copy.start()

    def block_copy(j):
        return pltpu.make_async_copy(x_ref.at[:, pl.ds(pl.multiple_of(j * LANE, LANE), LANE)], own.at[j], sems.at[j])

    for j in range(blocks):
        block_copy(j).start()
    first_col = lax.axis_index("tx") * cols
    for copy in few:
        copy.wait()
    for which in range(views):
        weights, rise = view_terms(bearing_ref, class_ref, which, cols * tx)
        disp_out[which] = disp_ref[which]
        for tap in range(TAPS):
            terms_ref[which, tap] = jnp.full((SUB, LANE), weights[tap], jnp.float32)
        terms_ref[which, TAPS] = rise
        for t in range(1, tiles - 1):
            peak_ref[which, t] = jnp.full((SUB, LANE), -jnp.inf, jnp.float32)

    @pl.loop(0, blocks)
    def _(j):
        block_copy(j).wait()
        edge_ref[0, j] = own[j, 0 : 2 * SUB, :]
        edge_ref[1, j] = own[j, rows - 2 * SUB : rows, :]
        column = column_tile(first_col, j)
        for which in range(views):
            weights = [terms_ref[which, tap] for tap in range(TAPS)]
            ramp = terms_ref[which, TAPS] * column
            disp = disp_ref[which] - 1
            for t in range(1, tiles - 1):
                value = lifted_tile(weights, ramp, lambda tap: own[j, pl.ds(t * SUB + disp + tap, SUB), :])
                lifted_ref[which, j, t * SUB : (t + 1) * SUB, :] = value
                peak_ref[which, t] = jnp.maximum(peak_ref[which, t], value)


def edge_kernel(disp_ref, terms_ref, up_ref, down_ref, edge_ref, peak_ref, inner_ref, lifted_ref, sent_ref, ring, tall, *, ty):
    cols = up_ref.shape[1]
    blocks = cols // LANE
    views, tiles = peak_ref.shape[:2]
    place = lax.axis_index("ty")
    first_col = lax.axis_index("tx") * cols
    for j in range(blocks):
        span = slice(j * LANE, (j + 1) * LANE)
        ring[0, j, 0:SUB, :] = jnp.where(place == 0, 0.0, up_ref[:, span])
        ring[0, j, SUB : 3 * SUB, :] = edge_ref[0, j]
        ring[1, j, 0 : 2 * SUB, :] = edge_ref[1, j]
        ring[1, j, 2 * SUB : 3 * SUB, :] = jnp.where(place == ty - 1, 0.0, down_ref[:, span])
    for which in range(views):
        weights, rise = [terms_ref[which, tap] for tap in range(TAPS)], terms_ref[which, TAPS]
        disp = disp_ref[which] - 1
        tops = []
        for end in range(2):
            top = None
            for j in range(blocks):
                value = lifted_tile(
                    weights,
                    rise * column_tile(first_col, j),
                    lambda tap: ring[end, j, pl.ds(SUB + disp + tap, SUB), :],
                )
                first = end * (tiles - 1) * SUB
                lifted_ref[which, j, first : first + SUB, :] = value
                top = value if top is None else jnp.maximum(top, value)
            tops.append(top)
        tall[0:SUB, :] = tops[0]
        for t in range(1, tiles - 1):
            tall[t * SUB : (t + 1) * SUB, :] = peak_ref[which, t]
        tall[(tiles - 1) * SUB : tiles * SUB, :] = tops[1]
        sent_ref[which : which + 1, :] = jnp.max(jnp.transpose(tall[...]), axis=0, keepdims=True)


def late_kernel(lifted_ref, margin_ref, turned, back):
    views, blocks, rows = lifted_ref.shape[:3]
    units = [(which, j) for which in range(views) for j in range(blocks)]
    lowest = jnp.full((SUB, rows), -jnp.inf, jnp.float32)
    carried = {}
    for n in range(len(units) + 2 * DELAY):
        if n < len(units):
            which, j = units[n]
            turned[which, j] = jnp.transpose(lifted_ref[which, j])
        if DELAY <= n < len(units) + DELAY:
            which, j = units[n - DELAY]
            if j == 0:
                carried = {1: lowest, 2: lowest, 4: lowest}
                peak = lowest
            tiles = [turned[which, j, i : i + SUB, :] for i in range(0, LANE, SUB)]
            for i, tile in enumerate(windows(tiles, carried)):
                peak = jnp.maximum(peak, tile)
                back[which, j, i * SUB : (i + 1) * SUB, :] = peak - tiles[i]
        if 2 * DELAY <= n:
            which, j = units[n - 2 * DELAY]
            margin_ref[which, j] = jnp.transpose(back[which, j])


def final_kernel(*refs, tx):
    partner_ref, *got_refs = refs[: tx // 2]
    lifted_ref, margin_ref, out_ref, stage, tall, sems = refs[tx // 2 :]
    views, rows, cols = out_ref.shape
    blocks, tiles = cols // LANE, rows // SUB
    place = lax.axis_index("tx")
    chip = place // 2
    before = jnp.where(lax.rem(place, 2) == 1, partner_ref[...], -jnp.inf)
    for i, got_ref in enumerate(got_refs):
        before = jnp.maximum(before, jnp.where((chip ^ (i + 1)) < chip, got_ref[...], -jnp.inf))
    for which in range(views):
        tall[which] = jnp.transpose(jnp.broadcast_to(before[which : which + 1, :], (LANE, rows)))
    copies = []
    for which in range(views):

        @pl.loop(0, tiles)
        def _(t):
            span = pl.ds(t * SUB, SUB)
            top = tall[which, span, :]
            for j in range(blocks):
                stage[which, span, j * LANE : (j + 1) * LANE] = jnp.maximum(
                    margin_ref[which, j, span, :], top - lifted_ref[which, j, span, :]
                )

        copies.append(pltpu.make_async_copy(stage.at[which], out_ref.at[which], sems.at[which]))
        copies[-1].start()
    for copy in copies:
        copy.wait()


def on_device(ty, tx, surface, bearing, disp, altitude):
    rows, cols = surface.shape
    views = bearing.shape[0]
    tiles, blocks = rows // SUB, cols // LANE
    f32 = jnp.float32
    assert tx & (tx - 1) == 0 and tx > 1
    up = lax.ppermute(surface[rows - SUB :], "ty", [(i, (i + 1) % ty) for i in range(ty)])
    down = lax.ppermute(surface[:SUB], "ty", [((i + 1) % ty, i) for i in range(ty)])
    smem = pl.BlockSpec(memory_space=pltpu.SMEM)
    vmem = pl.BlockSpec(memory_space=pltpu.VMEM)
    hbm = pl.BlockSpec(memory_space=pltpu.HBM)
    tile = (SUB, LANE)
    block_shape = (views, blocks, rows, LANE)
    pinned = [pltpu.with_memory_space_constraint(a, pltpu.HBM) for a in (bearing, disp, altitude, surface)]
    lifted, edge, peak, terms, shifts = pl.pallas_call(
        functools.partial(inner_kernel, tx=tx),
        out_shape=(
            pltpu.VMEM(block_shape, f32),
            pltpu.VMEM((2, blocks, 2 * SUB, LANE), f32),
            pltpu.VMEM((views, tiles) + tile, f32),
            pltpu.VMEM((views, TAPS + 1) + tile, f32),
            pltpu.SMEM((views,), jnp.int32),
        ),
        in_specs=[hbm] * 4,
        out_specs=[vmem] * 4 + [smem],
        scratch_shapes=[
            pltpu.VMEM((blocks, rows, LANE), f32),
            pltpu.SMEM((views,), jnp.int32),
            pltpu.SMEM((views,), jnp.int32),
            pltpu.SMEM((views,), jnp.int32),
            pltpu.SemaphoreType.DMA((blocks,)),
            pltpu.SemaphoreType.DMA((3,)),
        ],
        compiler_params=pltpu.CompilerParams(vmem_limit_bytes=16 * MIB),
        cost_estimate=pl.CostEstimate(flops=views * rows * cols * 40, bytes_accessed=rows * cols * 4, transcendentals=0),
        name="inner",
    )(*pinned)
    lifted, peaks = pl.pallas_call(
        functools.partial(edge_kernel, ty=ty),
        out_shape=(pltpu.VMEM(block_shape, f32), pltpu.VMEM((views, rows), f32)),
        in_specs=[smem] + [vmem] * 5 + [pl.BlockSpec(memory_space=pl.ANY)],
        out_specs=[vmem] * 2,
        scratch_shapes=[pltpu.VMEM((2, blocks, 3 * SUB, LANE), f32), pltpu.VMEM((rows, LANE), f32)],
        compiler_params=pltpu.CompilerParams(vmem_limit_bytes=16 * MIB),
        input_output_aliases={6: 0},
        name="edges",
    )(shifts, terms, up, down, edge, peak, lifted)
    partner = lax.ppermute(peaks, "tx", [(i, i ^ 1) for i in range(tx)])
    chip_peaks = jnp.maximum(peaks, partner)
    got = [lax.ppermute(chip_peaks, "tx", [(i, i ^ m) for i in range(tx)]) for m in range(2, tx, 2)]
    margin = pl.pallas_call(
        late_kernel,
        out_shape=pltpu.VMEM(block_shape, f32),
        in_specs=[vmem],
        out_specs=vmem,
        scratch_shapes=[pltpu.VMEM((views, blocks, LANE, rows), f32)] * 2,
        compiler_params=pltpu.CompilerParams(vmem_limit_bytes=24 * MIB),
        cost_estimate=pl.CostEstimate(flops=views * rows * cols * 40, bytes_accessed=rows * cols * 4, transcendentals=0),
        name="late",
    )(lifted)
    return pl.pallas_call(
        functools.partial(final_kernel, tx=tx),
        out_shape=jax.ShapeDtypeStruct((views, rows, cols), f32),
        in_specs=[vmem] * (tx // 2 + 2),
        out_specs=hbm,
        scratch_shapes=[
            pltpu.VMEM((views, rows, cols), f32),
            pltpu.VMEM((views, rows, LANE), f32),
            pltpu.SemaphoreType.DMA((views,)),
        ],
        compiler_params=pltpu.CompilerParams(vmem_limit_bytes=16 * MIB),
        name="finish",
    )(partner, *got, lifted, margin)


def solution(mesh):
    return jax.shard_map(
        functools.partial(on_device, mesh.shape["ty"], mesh.shape["tx"]),
        mesh=mesh,
        in_specs=(P("ty", "tx"), P(), P(), P()),
        out_specs=P(None, "ty", "tx"),
        check_vma=False,
    )
```

time: 24.7 us -> 22.4 us (0.907)
  Pallas kernels: 13.4 us -> 7.65 us
  waiting for transfers between devices: 1.74 us -> 5.14 us
    pallas_call x1, Pallas kernels: 6.16 us -> 2.24 us  [on_device(): pl.pallas_call(late_kernel, out_shape=pltpu.VMEM(block_shape, f32), in_sp...]
    pallas_call x1, Pallas kernels: 4.57 us -> 2.59 us  [on_device(): pl.pallas_call(functools.partial(inner_kernel, tx=tx), out_shape=(pltpu.V...]
    ppermute x1, waiting for transfers between devices: 0.58 us -> 2.55 us  [on_device(): lax.ppermute(surface[rows - SUB:], 'ty', [(i, (i + 1) % ty) for i in rang...]
    ppermute x3, waiting for transfers between devices: 0.01 us -> 1.44 us  [on_device(): lax.ppermute(chip_peaks, 'tx', [(i, i ^ m) for i in range(tx)])]
  transfers between devices with their start and end apart: 6 -> 6, of which waited for: 2 -> 3; matrix products, arithmetic and copies ran while one was open for 0% -> 0% of each run, Pallas kernels for 44% -> 22%
where the time goes in v3:
time: 22.4 us; the launch traced here: 22.2 us
  starting transfers between devices  8.44 us (38%)
  Pallas kernels  7.65 us (34%)
  waiting for transfers between devices  5.14 us (23%)
  local copies, waits for them, and re-layouts  0.88 us (4%)
    ppermute x3, starting transfers between devices, on_device(): lax.ppermute(chip_peaks, 'tx', [(i, i ^ m) for i in range(tx)])  4.39 us
    ppermute x1, starting transfers between devices, on_device(): lax.ppermute(surface[:SUB], 'ty', [((i + 1) % ty, i) for i in range(ty)])  3.97 us
    pallas_call x1, Pallas kernels, on_device(): pl.pallas_call(functools.partial(inner_kernel, tx=tx), out_shape=(pltpu.V...  2.59 us
    ppermute x1, waiting for transfers between devices, on_device(): lax.ppermute(surface[rows - SUB:], 'ty', [(i, (i + 1) % ty) for i in rang...  2.55 us
    pallas_call x1, Pallas kernels, on_device(): pl.pallas_call(functools.partial(final_kernel, tx=tx), out_shape=jax.Shap...  2.52 us
    pallas_call x1, Pallas kernels, on_device(): pl.pallas_call(late_kernel, out_shape=pltpu.VMEM(block_shape, f32), in_sp...  2.24 us
    ppermute x3, waiting for transfers between devices, on_device(): lax.ppermute(chip_peaks, 'tx', [(i, i ^ m) for i in range(tx)])  1.44 us
    ppermute x1, waiting for transfers between devices, on_device(): partner = lax.ppermute(peaks, 'tx', [(i, i ^ 1) for i in range(tx)])  1.15 us
  transfers between devices with their start and end apart: 6, of which 3 were waited for; matrix products, arithmetic and copies ran while one was open for 0% of the time, Pallas kernels for 22%

profile of v3, /device:TPU:0, one launch (start us, length us, event | category | flops | bytes accessed | tf_op | source)
XLA Modules:
  0.0 22.2 jit_solution(7364331970967953339)
XLA Ops:
  0.0 0.9 %fusion = (f32[8,2048]{1,0:T(8,128)S(1)}, f32[8,2048]{1,0:T(8,128)S(1)}) fusion(f32[128,2048]{1,0:T(8,128)} %x_ref.1), kind=kLoop, calls=%fused_computation | loop fusion | bytes 262144 | tf_op jit(solution)/shard_map/slice | solution.py:201
  0.9 4.0 %collective-permute-start.1 = (f32[8,2048]{1,0:T(8,128)S(1)}, f32[8,2048]{1,0:T(8,128)S(1)}, u32[]{:S(2)}, u32[]{:S(2)}) collective-permute-start(f32[8,2048]{1,0:T(8,128)S(1)} %get-tuple-element.19), channel_id=1, source_target_pairs={{8,0},{16,8},{24,16},{0,24},{9,1},{17,9},{25,17},{1,25},{10,2},{18... | collective-permute-start | bytes 196616 | tf_op jit(solution)/shard_map/ppermute | solution.py:201
  4.9 0.0 collective-permute-start
  4.9 2.6 %inner.1 = (f32[4,16,128,128]{3,2,1,0:T(8,128)S(1)}, f32[2,16,16,128]{3,2,1,0:T(8,128)S(1)}, f32[4,16,8,128]{3,2,1,0:T(8,128)S(1)}, f32[4,5,8,128]{3,2,1,0:T(8,128)S(1)}, s32[4]{0:T(128)S(4)}) custom-call(s32[4]{0:T(128)} %bearing_hbm.1, s32[4]{0:T(128)} %disp_hbm.1, s32[4]{0:T(128)} %class_hbm.1, f32[128,2048]{1,0:T(8,128)} %x_ref.1), custom_call_target="tpu_custom_call" | custom-call | flops 41943040 | bytes 1048576 | tf_op jit(solution)/shard_map/inner/pallas_call | solution.py:208
  7.5 0.0 collective-permute-done.1.down_ref
  7.5 2.5 %collective-permute-done.up_ref = f32[8,2048]{1,0:T(8,128)S(1)} collective-permute-done((f32[8,2048]{1,0:T(8,128)S(1)}, f32[8,2048]{1,0:T(8,128)S(1)}, u32[]{:S(2)}, u32[]{:S(2)}) %collective-permute-start) | collective-permute-done | bytes 65568 | tf_op jit(solution)/shard_map/ppermute | solution.py:200
  10.0 0.3 %edges.1 = (f32[4,16,128,128]{3,2,1,0:T(8,128)S(1)}, f32[4,128]{1,0:T(4,128)S(1)}) custom-call(s32[4]{0:T(128)S(4)} %get-tuple-element.12.disp_ref, f32[4,5,8,128]{3,2,1,0:T(8,128)S(1)} %get-tuple-element.13.terms_ref, f32[8,2048]{1,0:T(8,128)S(1)} %collective-permute-done.up_ref, ...), custom_call_target="tpu_custom_call", output_to_operand_aliasing={{0}: (6, {})} | custom-call | tf_op jit(solution)/shard_map/edges/pallas_call | solution.py:231
  10.3 0.1 collective-permute-start.2
  10.4 1.1 %collective-permute-done.2.refs_0_ = f32[4,128]{1,0:T(4,128)S(1)} collective-permute-done((f32[4,128]{1,0:T(4,128)S(1)}, f32[4,128]{1,0:T(4,128)S(1)}, u32[]{:S(2)}, u32[]{:S(2)}) %collective-permute-start.2) | collective-permute-done | bytes 2080 | tf_op jit(solution)/shard_map/ppermute | solution.py:241
  11.5 3.6 %collective-permute-start.5 = (f32[4,128]{1,0:T(4,128)S(1)}, f32[4,128]{1,0:T(4,128)S(1)}, u32[]{:S(2)}, u32[]{:S(2)}) collective-permute-start(f32[4,128]{1,0:T(4,128)S(1)} %max.3), channel_id=1, source_target_pairs={{0,6},{1,7},{2,4},{3,5},{4,2},{5,3},{6,0},{7,1},{8,14},{9,15},{10,... | collective-permute-start | bytes 6152 | tf_op jit(solution)/shard_map/ppermute | solution.py:243
  15.1 0.0 collective-permute-start.4
  15.2 0.8 %collective-permute-start.3 = (f32[4,128]{1,0:T(4,128)S(1)}, f32[4,128]{1,0:T(4,128)S(1)}, u32[]{:S(2)}, u32[]{:S(2)}) collective-permute-start(f32[4,128]{1,0:T(4,128)S(1)} %max.3), channel_id=1, source_target_pairs={{0,2},{1,3},{2,0},{3,1},{4,6},{5,7},{6,4},{7,5},{8,10},{9,11},{10,... | collective-permute-start | bytes 6152 | tf_op jit(solution)/shard_map/ppermute | solution.py:243
  15.9 2.2 %late.1.refs_5_ = f32[4,16,128,128]{3,2,1,0:T(8,128)S(1)} custom-call(f32[4,16,128,128]{3,2,1,0:T(8,128)S(1)} %get-tuple-element.18.lifted_ref.refs_4_), custom_call_target="tpu_custom_call" | custom-call | flops 41943040 | bytes 1048576 | tf_op jit(solution)/shard_map/late/pallas_call | solution.py:244
  18.2 0.0 collective-permute-done.5.refs_3_
  18.2 1.4 %collective-permute-done.4.refs_2_ = f32[4,128]{1,0:T(4,128)S(1)} collective-permute-done((f32[4,128]{1,0:T(4,128)S(1)}, f32[4,128]{1,0:T(4,128)S(1)}, u32[]{:S(2)}, u32[]{:S(2)}) %collective-permute-start.4) | collective-permute-done | bytes 2080 | tf_op jit(solution)/shard_map/ppermute | solution.py:243
  19.6 0.0 collective-permute-done.3.refs_1_
  19.6 2.5 %finish.1 = f32[4,128,2048]{2,1,0:T(8,128)} custom-call(f32[4,128]{1,0:T(4,128)S(1)} %collective-permute-done.2.refs_0_, f32[4,128]{1,0:T(4,128)S(1)} %collective-permute-done.3.refs_1_, f32[4,128]{1,0:T(4,128)S(1)} %collective-permute-done.4.refs_2_, f32[4,128]{1,0:T(4,128)S(1)} %collective-permute-done.5.refs_3_, ...), custom_call_target="tpu_custom_call" | custom-call | tf_op jit(solution)/shard_map/finish/pallas_call | solution.py:254
  (1 shorter events, 0.0 us)
Async XLA Ops:
  0.9 6.6 %collective-permute-start.1 = (f32[8,2048]{1,0:T(8,128)S(1)}, f32[8,2048]{1,0:T(8,128)S(1)}, u32[]{:S(2)}, u32[]{:S(2)}) collective-permute-start(f32[8,2048]{1,0:T(8,128)S(1)} %get-tuple-element.19), channel_id=1, source_target_pairs={{8,0},{16,8},{24,16},{0,24},{9,1},{17,9},{25,17},{1,25},{10,2},{18... | collective-permute-start | bytes 196616 | tf_op jit(solution)/shard_map/ppermute | solution.py:201
  4.9 5.2 %collective-permute-start = (f32[8,2048]{1,0:T(8,128)S(1)}, f32[8,2048]{1,0:T(8,128)S(1)}, u32[]{:S(2)}, u32[]{:S(2)}) collective-permute-start(f32[8,2048]{1,0:T(8,128)S(1)} %get-tuple-element.20), channel_id=1, source_target_pairs={{0,8},{8,16},{16,24},{24,0},{1,9},{9,17},{17,25},{25,1},{2,10},{10... | collective-permute-start | bytes 196616 | tf_op jit(solution)/shard_map/ppermute | solution.py:200
  10.3 1.2 %collective-permute-start.2 = (f32[4,128]{1,0:T(4,128)S(1)}, f32[4,128]{1,0:T(4,128)S(1)}, u32[]{:S(2)}, u32[]{:S(2)}) collective-permute-start(f32[4,128]{1,0:T(4,128)S(1)} %get-tuple-element.17), channel_id=1, source_target_pairs={{0,1},{1,0},{2,3},{3,2},{4,5},{5,4},{6,7},{7,6},{8,9},{9,8},{10,11... | collective-permute-start | bytes 6152 | tf_op jit(solution)/shard_map/ppermute | solution.py:241
  11.5 6.6 %collective-permute-start.5 = (f32[4,128]{1,0:T(4,128)S(1)}, f32[4,128]{1,0:T(4,128)S(1)}, u32[]{:S(2)}, u32[]{:S(2)}) collective-permute-start(f32[4,128]{1,0:T(4,128)S(1)} %max.3), channel_id=1, source_target_pairs={{0,6},{1,7},{2,4},{3,5},{4,2},{5,3},{6,0},{7,1},{8,14},{9,15},{10,... | collective-permute-start | bytes 6152 | tf_op jit(solution)/shard_map/ppermute | solution.py:243
  15.1 4.5 %collective-permute-start.4 = (f32[4,128]{1,0:T(4,128)S(1)}, f32[4,128]{1,0:T(4,128)S(1)}, u32[]{:S(2)}, u32[]{:S(2)}) collective-permute-start(f32[4,128]{1,0:T(4,128)S(1)} %max.3), channel_id=1, source_target_pairs={{0,4},{1,5},{2,6},{3,7},{4,0},{5,1},{6,2},{7,3},{8,12},{9,13},{10,... | collective-permute-start | bytes 6152 | tf_op jit(solution)/shard_map/ppermute | solution.py:243
  15.2 4.5 %collective-permute-start.3 = (f32[4,128]{1,0:T(4,128)S(1)}, f32[4,128]{1,0:T(4,128)S(1)}, u32[]{:S(2)}, u32[]{:S(2)}) collective-permute-start(f32[4,128]{1,0:T(4,128)S(1)} %max.3), channel_id=1, source_target_pairs={{0,2},{1,3},{2,0},{3,1},{4,6},{5,7},{6,4},{7,5},{8,10},{9,11},{10,... | collective-permute-start | bytes 6152 | tf_op jit(solution)/shard_map/ppermute | solution.py:243

commit v4 on v3

--- a/solution.py
+++ b/solution.py
@@ -12,6 +12,9 @@
 SUB = 8
 LANE = 128
 MIB = 1 << 20
+REACH = 4
+ABOVE, BELOW = REACH + 1, REACH + 2
+CHUNKS = 4
 DELAY = 2
 
 
@@ -56,34 +59,47 @@
     return tiles
 
 
-def inner_kernel(
-    bearing_hbm, disp_hbm, class_hbm, x_ref, lifted_ref, edge_ref, peak_ref, terms_ref, disp_out,
-    own, bearing_ref, disp_ref, class_ref, sems, few_sems, *, tx,
+def prepare_kernel(
+    bearing_hbm, disp_hbm, class_hbm, x_ref, tail_ref, head_ref, terms_ref, disp_out,
+    ends, bearing_ref, disp_ref, class_ref, end_sems, sems, *, tx,
 ):
     rows, cols = x_ref.shape
-    blocks, tiles = cols // LANE, rows // SUB
-    views = bearing_ref.shape[0]
-    few = [
-        pltpu.make_async_copy(source, target, few_sems.at[i])
+    blocks = cols // LANE
+    copies = [
+        pltpu.make_async_copy(x_ref.at[pl.ds(first, SUB)], ends.at[end], end_sems.at[end])
+        for end, first in enumerate((rows - SUB, 0))
+    ] + [
+        pltpu.make_async_copy(source, target, sems.at[i])
         for i, (source, target) in enumerate(((bearing_hbm, bearing_ref), (disp_hbm, disp_ref), (class_hbm, class_ref)))
     ]
-    for copy in few:
+    for copy in copies:
         copy.start()
-
-    def block_copy(j):
-        return pltpu.make_async_copy(x_ref.at[:, pl.ds(pl.multiple_of(j * LANE, LANE), LANE)], own.at[j], sems.at[j])
-
+    for copy in copies:
+        copy.wait()
     for j in range(blocks):
-        block_copy(j).start()
-    first_col = lax.axis_index("tx") * cols
-    for copy in few:
-        copy.wait()
-    for which in range(views):
+        span = slice(j * LANE, (j + 1) * LANE)
+        tail_ref[j * ABOVE : (j + 1) * ABOVE, :] = ends[0, SUB - ABOVE : SUB, span]
+        head_ref[j * BELOW : (j + 1) * BELOW, :] = ends[1, 0:BELOW, span]
+    for which in range(bearing_ref.shape[0]):
         weights, rise = view_terms(bearing_ref, class_ref, which, cols * tx)
         disp_out[which] = disp_ref[which]
         for tap in range(TAPS):
             terms_ref[which, tap] = jnp.full((SUB, LANE), weights[tap], jnp.float32)
         terms_ref[which, TAPS] = rise
+
+
+def inner_kernel(disp_ref, terms_ref, x_ref, lifted_ref, edge_ref, peak_ref, own, sems):
+    rows, cols = x_ref.shape
+    blocks, tiles = cols // LANE, rows // SUB
+    views = terms_ref.shape[0]
+
+    def block_copy(j):
+        return pltpu.make_async_copy(x_ref.at[:, pl.ds(pl.multiple_of(j * LANE, LANE), LANE)], own.at[j], sems.at[j])
+
+    for j in range(blocks):
+        block_copy(j).start()
+    first_col = lax.axis_index("tx") * cols
+    for which in range(views):
         for t in range(1, tiles - 1):
             peak_ref[which, t] = jnp.full((SUB, LANE), -jnp.inf, jnp.float32)
 
@@ -104,17 +120,18 @@
 
 
 def edge_kernel(disp_ref, terms_ref, up_ref, down_ref, edge_ref, peak_ref, inner_ref, lifted_ref, sent_ref, ring, tall, *, ty):
-    cols = up_ref.shape[1]
-    blocks = cols // LANE
+    blocks = edge_ref.shape[1]
+    cols = blocks * LANE
     views, tiles = peak_ref.shape[:2]
     place = lax.axis_index("ty")
     first_col = lax.axis_index("tx") * cols
     for j in range(blocks):
-        span = slice(j * LANE, (j + 1) * LANE)
-        ring[0, j, 0:SUB, :] = jnp.where(place == 0, 0.0, up_ref[:, span])
+        above = up_ref[j * ABOVE : (j + 1) * ABOVE, :]
+        below = down_ref[j * BELOW : (j + 1) * BELOW, :]
+        ring[0, j, SUB - ABOVE : SUB, :] = jnp.where(place == 0, 0.0, above)
         ring[0, j, SUB : 3 * SUB, :] = edge_ref[0, j]
         ring[1, j, 0 : 2 * SUB, :] = edge_ref[1, j]
-        ring[1, j, 2 * SUB : 3 * SUB, :] = jnp.where(place == ty - 1, 0.0, down_ref[:, span])
+        ring[1, j, 2 * SUB : 2 * SUB + BELOW, :] = jnp.where(place == ty - 1, 0.0, below)
     for which in range(views):
         weights, rise = [terms_ref[which, tap] for tap in range(TAPS)], terms_ref[which, TAPS]
         disp = disp_ref[which] - 1
@@ -173,20 +190,22 @@
         before = jnp.maximum(before, jnp.where((chip ^ (i + 1)) < chip, got_ref[...], -jnp.inf))
     for which in range(views):
         tall[which] = jnp.transpose(jnp.broadcast_to(before[which : which + 1, :], (LANE, rows)))
+    chunk = rows // CHUNKS
     copies = []
     for which in range(views):
-
-        @pl.loop(0, tiles)
-        def _(t):
-            span = pl.ds(t * SUB, SUB)
-            top = tall[which, span, :]
-            for j in range(blocks):
-                stage[which, span, j * LANE : (j + 1) * LANE] = jnp.maximum(
-                    margin_ref[which, j, span, :], top - lifted_ref[which, j, span, :]
-                )
-
-        copies.append(pltpu.make_async_copy(stage.at[which], out_ref.at[which], sems.at[which]))
-        copies[-1].start()
+        for first in range(0, rows, chunk):
+            for t in range(first, first + chunk, SUB):
+                span = slice(t, t + SUB)
+                top = tall[which, span, :]
+                for j in range(blocks):
+                    stage[which, span, j * LANE : (j + 1) * LANE] = jnp.maximum(
+                        margin_ref[which, j, span, :], top - lifted_ref[which, j, span, :]
+                    )
+            part = pl.ds(first, chunk)
+            copies.append(
+                pltpu.make_async_copy(stage.at[which, part], out_ref.at[which, part], sems.at[which, first // chunk])
+            )
+            copies[-1].start()
     for copy in copies:
         copy.wait()
 
@@ -197,37 +216,49 @@
     tiles, blocks = rows // SUB, cols // LANE
     f32 = jnp.float32
     assert tx & (tx - 1) == 0 and tx > 1
-    up = lax.ppermute(surface[rows - SUB :], "ty", [(i, (i + 1) % ty) for i in range(ty)])
-    down = lax.ppermute(surface[:SUB], "ty", [((i + 1) % ty, i) for i in range(ty)])
     smem = pl.BlockSpec(memory_space=pltpu.SMEM)
     vmem = pl.BlockSpec(memory_space=pltpu.VMEM)
     hbm = pl.BlockSpec(memory_space=pltpu.HBM)
     tile = (SUB, LANE)
     block_shape = (views, blocks, rows, LANE)
     pinned = [pltpu.with_memory_space_constraint(a, pltpu.HBM) for a in (bearing, disp, altitude, surface)]
-    lifted, edge, peak, terms, shifts = pl.pallas_call(
-        functools.partial(inner_kernel, tx=tx),
+    tail, head, terms, shifts = pl.pallas_call(
+        functools.partial(prepare_kernel, tx=tx),
+        out_shape=(
+            pltpu.VMEM((blocks * ABOVE, LANE), f32),
+            pltpu.VMEM((blocks * BELOW, LANE), f32),
+            pltpu.VMEM((views, TAPS + 1) + tile, f32),
+            pltpu.SMEM((views,), jnp.int32),
+        ),
+        in_specs=[hbm] * 4,
+        out_specs=[vmem] * 3 + [smem],
+        scratch_shapes=[
+            pltpu.VMEM((2, SUB, cols), f32),
+            pltpu.SMEM((views,), jnp.int32),
+            pltpu.SMEM((views,), jnp.int32),
+            pltpu.SMEM((views,), jnp.int32),
+            pltpu.SemaphoreType.DMA((2,)),
+            pltpu.SemaphoreType.DMA((3,)),
+        ],
+        compiler_params=pltpu.CompilerParams(vmem_limit_bytes=8 * MIB),
+        name="prepare",
+    )(*pinned)
+    up = lax.ppermute(tail, "ty", [(i, (i + 1) % ty) for i in range(ty)])
+    down = lax.ppermute(head, "ty", [((i + 1) % ty, i) for i in range(ty)])
+    lifted, edge, peak = pl.pallas_call(
+        inner_kernel,
         out_shape=(
             pltpu.VMEM(block_shape, f32),
             pltpu.VMEM((2, blocks, 2 * SUB, LANE), f32),
             pltpu.VMEM((views, tiles) + tile, f32),
-            pltpu.VMEM((views, TAPS + 1) + tile, f32),
-            pltpu.SMEM((views,), jnp.int32),
         ),
-        in_specs=[hbm] * 4,
-        out_specs=[vmem] * 4 + [smem],
-        scratch_shapes=[
-            pltpu.VMEM((blocks, rows, LANE), f32),
-            pltpu.SMEM((views,), jnp.int32),
-            pltpu.SMEM((views,), jnp.int32),
-            pltpu.SMEM((views,), jnp.int32),
-            pltpu.SemaphoreType.DMA((blocks,)),
-            pltpu.SemaphoreType.DMA((3,)),
-        ],
+        in_specs=[smem, vmem, hbm],
+        out_specs=[vmem] * 3,
+        scratch_shapes=[pltpu.VMEM((blocks, rows, LANE), f32), pltpu.SemaphoreType.DMA((blocks,))],
         compiler_params=pltpu.CompilerParams(vmem_limit_bytes=16 * MIB),
         cost_estimate=pl.CostEstimate(flops=views * rows * cols * 40, bytes_accessed=rows * cols * 4, transcendentals=0),
         name="inner",
-    )(*pinned)
+    )(shifts, terms, pinned[3])
     lifted, peaks = pl.pallas_call(
         functools.partial(edge_kernel, ty=ty),
         out_shape=(pltpu.VMEM(block_shape, f32), pltpu.VMEM((views, rows), f32)),
@@ -259,7 +290,7 @@
         scratch_shapes=[
             pltpu.VMEM((views, rows, cols), f32),
             pltpu.VMEM((views, rows, LANE), f32),
-            pltpu.SemaphoreType.DMA((views,)),
+            pltpu.SemaphoreType.DMA((views, CHUNKS)),
         ],
         compiler_params=pltpu.CompilerParams(vmem_limit_bytes=16 * MIB),
         name="finish",

time: 22.4 us -> 22 us (0.982)
  local copies, waits for them, and re-layouts: 0.88 us -> 0 us
  Pallas kernels: 7.65 us -> 8.28 us
    pallas_call x1 -> x2, Pallas kernels: 2.59 us -> 3.48 us  [the longest x1 2.44 us: on_device(): pl.pallas_call(inner_kernel, out_shape=(pltpu.VMEM(block_shape, f32), plt...]
    slice x1 -> x0, local copies, waits for them, and re-layouts: 0.88 us -> none  [on_device(): surface[:SUB]]
    pallas_call x1, Pallas kernels: 2.52 us -> 2.26 us  [on_device(): pl.pallas_call(functools.partial(final_kernel, tx=tx), out_shape=jax.Shap...]
  transfers between devices with their start and end apart: 6 -> 6, of which waited for: 3 -> 3; matrix products, arithmetic and copies ran while one was open for 0% -> 0% of each run, Pallas kernels for 22% -> 21%
where the time goes in v4:
time: 22 us; the launch traced here: 21.8 us
  starting transfers between devices  8.44 us (38%)
  Pallas kernels  8.28 us (38%)
  waiting for transfers between devices  5.05 us (23%)
    ppermute x3, starting transfers between devices, on_device(): lax.ppermute(chip_peaks, 'tx', [(i, i ^ m) for i in range(tx)])  4.39 us
    ppermute x1, starting transfers between devices, on_device(): down = lax.ppermute(head, 'ty', [((i + 1) % ty, i) for i in range(ty)])  3.97 us
    ppermute x1, waiting for transfers between devices, on_device(): up = lax.ppermute(tail, 'ty', [(i, (i + 1) % ty) for i in range(ty)])  2.45 us
    pallas_call x1, Pallas kernels, on_device(): pl.pallas_call(inner_kernel, out_shape=(pltpu.VMEM(block_shape, f32), plt...  2.44 us
    pallas_call x1, Pallas kernels, on_device(): pl.pallas_call(functools.partial(final_kernel, tx=tx), out_shape=jax.Shap...  2.26 us
    pallas_call x1, Pallas kernels, on_device(): pl.pallas_call(late_kernel, out_shape=pltpu.VMEM(block_shape, f32), in_sp...  2.24 us
    ppermute x3, waiting for transfers between devices, on_device(): lax.ppermute(chip_peaks, 'tx', [(i, i ^ m) for i in range(tx)])  1.44 us
    ppermute x1, waiting for transfers between devices, on_device(): partner = lax.ppermute(peaks, 'tx', [(i, i ^ 1) for i in range(tx)])  1.15 us
  transfers between devices with their start and end apart: 6, of which 3 were waited for; matrix products, arithmetic and copies ran while one was open for 0% of the time, Pallas kernels for 21%

profile of v4, /device:TPU:0, one launch (start us, length us, event | category | flops | bytes accessed | tf_op | source)
XLA Modules:
  0.0 21.8 jit_solution(12635668792075035368)
XLA Ops:
  0.0 1.0 %prepare.1 = (f32[80,128]{1,0:T(8,128)S(1)}, f32[96,128]{1,0:T(8,128)S(1)}, f32[4,5,8,128]{3,2,1,0:T(8,128)S(1)}, s32[4]{0:T(128)S(4)}) custom-call(s32[4]{0:T(128)} %bearing_hbm.1, s32[4]{0:T(128)} %disp_hbm.1, s32[4]{0:T(128)} %class_hbm.1, f32[128,2048]{1,0:T(8,128)} %x_ref.3), custom_call_target="tpu_custom_call" | custom-call | tf_op jit(solution)/shard_map/prepare/pallas_call | solution.py:225
  1.1 4.0 %collective-permute-start.1 = (f32[96,128]{1,0:T(8,128)S(1)}, f32[96,128]{1,0:T(8,128)S(1)}, u32[]{:S(2)}, u32[]{:S(2)}) collective-permute-start(f32[96,128]{1,0:T(8,128)S(1)} %get-tuple-element.17), channel_id=1, source_target_pairs={{8,0},{16,8},{24,16},{0,24},{9,1},{17,9},{25,17},{1,25},{10,2},{18... | collective-permute-start | bytes 147464 | tf_op jit(solution)/shard_map/ppermute | solution.py:247
  5.0 0.0 collective-permute-start
  5.0 2.4 %inner.1 = (f32[4,16,128,128]{3,2,1,0:T(8,128)S(1)}, f32[2,16,16,128]{3,2,1,0:T(8,128)S(1)}, f32[4,16,8,128]{3,2,1,0:T(8,128)S(1)}) custom-call(s32[4]{0:T(128)S(4)} %get-tuple-element.14.disp_ref, f32[4,5,8,128]{3,2,1,0:T(8,128)S(1)} %get-tuple-element.15.terms_ref, f32[128,2048]{1,0:T(8,128)} %x_ref.3), custom_call_target="tpu_custom_call" | custom-call | flops 41943040 | bytes 1048576 | tf_op jit(solution)/shard_map/inner/pallas_call | solution.py:248
  7.5 2.5 %collective-permute-done.up_ref = f32[80,128]{1,0:T(8,128)S(1)} collective-permute-done((f32[80,128]{1,0:T(8,128)S(1)}, f32[80,128]{1,0:T(8,128)S(1)}, u32[]{:S(2)}, u32[]{:S(2)}) %collective-permute-start) | collective-permute-done | bytes 40992 | tf_op jit(solution)/shard_map/ppermute | solution.py:246
  9.9 0.0 collective-permute-done.1.down_ref
  9.9 0.3 %edges.1 = (f32[4,16,128,128]{3,2,1,0:T(8,128)S(1)}, f32[4,128]{1,0:T(4,128)S(1)}) custom-call(s32[4]{0:T(128)S(4)} %get-tuple-element.14.disp_ref, f32[4,5,8,128]{3,2,1,0:T(8,128)S(1)} %get-tuple-element.15.terms_ref, f32[80,128]{1,0:T(8,128)S(1)} %collective-permute-done.up_ref, ...), custom_call_target="tpu_custom_call", output_to_operand_aliasing={{0}: (6, {})} | custom-call | tf_op jit(solution)/shard_map/edges/pallas_call | solution.py:262
  10.2 0.1 collective-permute-start.2
  10.3 1.1 %collective-permute-done.2.refs_0_ = f32[4,128]{1,0:T(4,128)S(1)} collective-permute-done((f32[4,128]{1,0:T(4,128)S(1)}, f32[4,128]{1,0:T(4,128)S(1)}, u32[]{:S(2)}, u32[]{:S(2)}) %collective-permute-start.2) | collective-permute-done | bytes 2080 | tf_op jit(solution)/shard_map/ppermute | solution.py:272
  11.5 3.6 %collective-permute-start.5 = (f32[4,128]{1,0:T(4,128)S(1)}, f32[4,128]{1,0:T(4,128)S(1)}, u32[]{:S(2)}, u32[]{:S(2)}) collective-permute-start(f32[4,128]{1,0:T(4,128)S(1)} %max.3), channel_id=1, source_target_pairs={{0,6},{1,7},{2,4},{3,5},{4,2},{5,3},{6,0},{7,1},{8,14},{9,15},{10,... | collective-permute-start | bytes 6152 | tf_op jit(solution)/shard_map/ppermute | solution.py:274
  15.1 0.0 collective-permute-start.4
  15.1 0.8 %collective-permute-start.3 = (f32[4,128]{1,0:T(4,128)S(1)}, f32[4,128]{1,0:T(4,128)S(1)}, u32[]{:S(2)}, u32[]{:S(2)}) collective-permute-start(f32[4,128]{1,0:T(4,128)S(1)} %max.3), channel_id=1, source_target_pairs={{0,2},{1,3},{2,0},{3,1},{4,6},{5,7},{6,4},{7,5},{8,10},{9,11},{10,... | collective-permute-start | bytes 6152 | tf_op jit(solution)/shard_map/ppermute | solution.py:274
  15.8 2.2 %late.1.refs_5_ = f32[4,16,128,128]{3,2,1,0:T(8,128)S(1)} custom-call(f32[4,16,128,128]{3,2,1,0:T(8,128)S(1)} %get-tuple-element.22.lifted_ref.refs_4_), custom_call_target="tpu_custom_call" | custom-call | flops 41943040 | bytes 1048576 | tf_op jit(solution)/shard_map/late/pallas_call | solution.py:275
  18.1 0.0 collective-permute-done.5.refs_3_
  18.1 1.4 %collective-permute-done.4.refs_2_ = f32[4,128]{1,0:T(4,128)S(1)} collective-permute-done((f32[4,128]{1,0:T(4,128)S(1)}, f32[4,128]{1,0:T(4,128)S(1)}, u32[]{:S(2)}, u32[]{:S(2)}) %collective-permute-start.4) | collective-permute-done | bytes 2080 | tf_op jit(solution)/shard_map/ppermute | solution.py:274
  19.5 0.0 collective-permute-done.3.refs_1_
  19.5 2.3 %finish.1 = f32[4,128,2048]{2,1,0:T(8,128)} custom-call(f32[4,128]{1,0:T(4,128)S(1)} %collective-permute-done.2.refs_0_, f32[4,128]{1,0:T(4,128)S(1)} %collective-permute-done.3.refs_1_, f32[4,128]{1,0:T(4,128)S(1)} %collective-permute-done.4.refs_2_, f32[4,128]{1,0:T(4,128)S(1)} %collective-permute-done.5.refs_3_, ...), custom_call_target="tpu_custom_call" | custom-call | tf_op jit(solution)/shard_map/finish/pallas_call | solution.py:285
  (1 shorter events, 0.0 us)
Async XLA Ops:
  1.1 8.9 %collective-permute-start.1 = (f32[96,128]{1,0:T(8,128)S(1)}, f32[96,128]{1,0:T(8,128)S(1)}, u32[]{:S(2)}, u32[]{:S(2)}) collective-permute-start(f32[96,128]{1,0:T(8,128)S(1)} %get-tuple-element.17), channel_id=1, source_target_pairs={{8,0},{16,8},{24,16},{0,24},{9,1},{17,9},{25,17},{1,25},{10,2},{18... | collective-permute-start | bytes 147464 | tf_op jit(solution)/shard_map/ppermute | solution.py:247
  5.0 4.9 %collective-permute-start = (f32[80,128]{1,0:T(8,128)S(1)}, f32[80,128]{1,0:T(8,128)S(1)}, u32[]{:S(2)}, u32[]{:S(2)}) collective-permute-start(f32[80,128]{1,0:T(8,128)S(1)} %get-tuple-element.16), channel_id=1, source_target_pairs={{0,8},{8,16},{16,24},{24,0},{1,9},{9,17},{17,25},{25,1},{2,10},{10... | collective-permute-start | bytes 122888 | tf_op jit(solution)/shard_map/ppermute | solution.py:246
  10.2 1.2 %collective-permute-start.2 = (f32[4,128]{1,0:T(4,128)S(1)}, f32[4,128]{1,0:T(4,128)S(1)}, u32[]{:S(2)}, u32[]{:S(2)}) collective-permute-start(f32[4,128]{1,0:T(4,128)S(1)} %get-tuple-element.21), channel_id=1, source_target_pairs={{0,1},{1,0},{2,3},{3,2},{4,5},{5,4},{6,7},{7,6},{8,9},{9,8},{10,11... | collective-permute-start | bytes 6152 | tf_op jit(solution)/shard_map/ppermute | solution.py:272
  11.5 6.6 %collective-permute-start.5 = (f32[4,128]{1,0:T(4,128)S(1)}, f32[4,128]{1,0:T(4,128)S(1)}, u32[]{:S(2)}, u32[]{:S(2)}) collective-permute-start(f32[4,128]{1,0:T(4,128)S(1)} %max.3), channel_id=1, source_target_pairs={{0,6},{1,7},{2,4},{3,5},{4,2},{5,3},{6,0},{7,1},{8,14},{9,15},{10,... | collective-permute-start | bytes 6152 | tf_op jit(solution)/shard_map/ppermute | solution.py:274
  15.1 4.5 %collective-permute-start.4 = (f32[4,128]{1,0:T(4,128)S(1)}, f32[4,128]{1,0:T(4,128)S(1)}, u32[]{:S(2)}, u32[]{:S(2)}) collective-permute-start(f32[4,128]{1,0:T(4,128)S(1)} %max.3), channel_id=1, source_target_pairs={{0,4},{1,5},{2,6},{3,7},{4,0},{5,1},{6,2},{7,3},{8,12},{9,13},{10,... | collective-permute-start | bytes 6152 | tf_op jit(solution)/shard_map/ppermute | solution.py:274
  15.1 4.5 %collective-permute-start.3 = (f32[4,128]{1,0:T(4,128)S(1)}, f32[4,128]{1,0:T(4,128)S(1)}, u32[]{:S(2)}, u32[]{:S(2)}) collective-permute-start(f32[4,128]{1,0:T(4,128)S(1)} %max.3), channel_id=1, source_target_pairs={{0,2},{1,3},{2,0},{3,1},{4,6},{5,7},{6,4},{7,5},{8,10},{9,11},{10,... | collective-permute-start | bytes 6152 | tf_op jit(solution)/shard_map/ppermute | solution.py:274

commit v5 on v4

--- a/solution.py
+++ b/solution.py
@@ -13,7 +13,7 @@
 LANE = 128
 MIB = 1 << 20
 REACH = 4
-ABOVE, BELOW = REACH + 1, REACH + 2
+BELOW = REACH + 2
 CHUNKS = 4
 DELAY = 2
 
@@ -60,11 +60,12 @@
 
 
 def prepare_kernel(
-    bearing_hbm, disp_hbm, class_hbm, x_ref, tail_ref, head_ref, terms_ref, disp_out,
+    bearing_hbm, disp_hbm, class_hbm, x_ref, near_ref, far_ref, terms_ref, disp_out,
     ends, bearing_ref, disp_ref, class_ref, end_sems, sems, *, tx,
 ):
     rows, cols = x_ref.shape
     blocks = cols // LANE
+    even = lax.rem(lax.axis_index("ty"), 2) == 0
     copies = [
         pltpu.make_async_copy(x_ref.at[pl.ds(first, SUB)], ends.at[end], end_sems.at[end])
         for end, first in enumerate((rows - SUB, 0))
@@ -78,8 +79,9 @@
         copy.wait()
     for j in range(blocks):
         span = slice(j * LANE, (j + 1) * LANE)
-        tail_ref[j * ABOVE : (j + 1) * ABOVE, :] = ends[0, SUB - ABOVE : SUB, span]
-        head_ref[j * BELOW : (j + 1) * BELOW, :] = ends[1, 0:BELOW, span]
+        tail, head = ends[0, SUB - BELOW : SUB, span], ends[1, 0:BELOW, span]
+        near_ref[j * BELOW : (j + 1) * BELOW, :] = jnp.where(even, tail, head)
+        far_ref[j * BELOW : (j + 1) * BELOW, :] = jnp.where(even, head, tail)
     for which in range(bearing_ref.shape[0]):
         weights, rise = view_terms(bearing_ref, class_ref, which, cols * tx)
         disp_out[which] = disp_ref[which]
@@ -119,16 +121,17 @@
                 peak_ref[which, t] = jnp.maximum(peak_ref[which, t], value)
 
 
-def edge_kernel(disp_ref, terms_ref, up_ref, down_ref, edge_ref, peak_ref, inner_ref, lifted_ref, sent_ref, ring, tall, *, ty):
+def edge_kernel(disp_ref, terms_ref, near_ref, far_ref, edge_ref, peak_ref, inner_ref, lifted_ref, sent_ref, ring, tall, *, ty):
     blocks = edge_ref.shape[1]
     cols = blocks * LANE
     views, tiles = peak_ref.shape[:2]
     place = lax.axis_index("ty")
+    even = lax.rem(place, 2) == 0
     first_col = lax.axis_index("tx") * cols
     for j in range(blocks):
-        above = up_ref[j * ABOVE : (j + 1) * ABOVE, :]
-        below = down_ref[j * BELOW : (j + 1) * BELOW, :]
-        ring[0, j, SUB - ABOVE : SUB, :] = jnp.where(place == 0, 0.0, above)
+        near, far = near_ref[j * BELOW : (j + 1) * BELOW, :], far_ref[j * BELOW : (j + 1) * BELOW, :]
+        above, below = jnp.where(even, far, near), jnp.where(even, near, far)
+        ring[0, j, SUB - BELOW : SUB, :] = jnp.where(place == 0, 0.0, above)
         ring[0, j, SUB : 3 * SUB, :] = edge_ref[0, j]
         ring[1, j, 0 : 2 * SUB, :] = edge_ref[1, j]
         ring[1, j, 2 * SUB : 2 * SUB + BELOW, :] = jnp.where(place == ty - 1, 0.0, below)
@@ -210,22 +213,33 @@
         copy.wait()
 
 
+def halo_pairs(ty, tx):
+    near, far = [], []
+    for row in range(ty):
+        for col in range(tx):
+            at = row * tx + col
+            near.append((at, (row ^ 1) * tx + col))
+            other = row - 1 if row % 2 == 0 else row + 1
+            far.append((at, other * tx + col if 0 <= other < ty else row * tx + (col ^ 1)))
+    return near, far
+
+
 def on_device(ty, tx, surface, bearing, disp, altitude):
     rows, cols = surface.shape
     views = bearing.shape[0]
     tiles, blocks = rows // SUB, cols // LANE
     f32 = jnp.float32
-    assert tx & (tx - 1) == 0 and tx > 1
+    assert tx & (tx - 1) == 0 and tx > 1 and ty % 2 == 0
     smem = pl.BlockSpec(memory_space=pltpu.SMEM)
     vmem = pl.BlockSpec(memory_space=pltpu.VMEM)
     hbm = pl.BlockSpec(memory_space=pltpu.HBM)
     tile = (SUB, LANE)
     block_shape = (views, blocks, rows, LANE)
     pinned = [pltpu.with_memory_space_constraint(a, pltpu.HBM) for a in (bearing, disp, altitude, surface)]
-    tail, head, terms, shifts = pl.pallas_call(
+    sends_near, sends_far, terms, shifts = pl.pallas_call(
         functools.partial(prepare_kernel, tx=tx),
         out_shape=(
-            pltpu.VMEM((blocks * ABOVE, LANE), f32),
+            pltpu.VMEM((blocks * BELOW, LANE), f32),
             pltpu.VMEM((blocks * BELOW, LANE), f32),
             pltpu.VMEM((views, TAPS + 1) + tile, f32),
             pltpu.SMEM((views,), jnp.int32),
@@ -243,8 +257,9 @@
         compiler_params=pltpu.CompilerParams(vmem_limit_bytes=8 * MIB),
         name="prepare",
     )(*pinned)
-    up = lax.ppermute(tail, "ty", [(i, (i + 1) % ty) for i in range(ty)])
-    down = lax.ppermute(head, "ty", [((i + 1) % ty, i) for i in range(ty)])
+    near, far = halo_pairs(ty, tx)
+    got_near = lax.ppermute(sends_near, ("ty", "tx"), near)
+    got_far = lax.ppermute(sends_far, ("ty", "tx"), far)
     lifted, edge, peak = pl.pallas_call(
         inner_kernel,
         out_shape=(
@@ -268,7 +283,7 @@
         compiler_params=pltpu.CompilerParams(vmem_limit_bytes=16 * MIB),
         input_output_aliases={6: 0},
         name="edges",
-    )(shifts, terms, up, down, edge, peak, lifted)
+    )(shifts, terms, got_near, got_far, edge, peak, lifted)
     partner = lax.ppermute(peaks, "tx", [(i, i ^ 1) for i in range(tx)])
     chip_peaks = jnp.maximum(peaks, partner)
     got = [lax.ppermute(chip_peaks, "tx", [(i, i ^ m) for i in range(tx)]) for m in range(2, tx, 2)]

time: 22 us -> 19.7 us (0.90)
  the two profiles are of different devices: /device:TPU:0 before, /device:TPU:4 now
where the time goes in v5:
time: 19.7 us; the launch traced here: 19.5 us
  Pallas kernels  8.22 us (42%)
  starting transfers between devices  6.04 us (31%)
  waiting for transfers between devices  5.17 us (26%)
    ppermute x3, starting transfers between devices, on_device(): lax.ppermute(chip_peaks, 'tx', [(i, i ^ m) for i in range(tx)])  4.39 us
    ppermute x1, waiting for transfers between devices, on_device(): got_far = lax.ppermute(sends_far, ('ty', 'tx'), far)  2.39 us
    pallas_call x1, Pallas kernels, on_device(): pl.pallas_call(inner_kernel, out_shape=(pltpu.VMEM(block_shape, f32), plt...  2.38 us
    pallas_call x1, Pallas kernels, on_device(): pl.pallas_call(functools.partial(final_kernel, tx=tx), out_shape=jax.Shap...  2.26 us
    pallas_call x1, Pallas kernels, on_device(): pl.pallas_call(late_kernel, out_shape=pltpu.VMEM(block_shape, f32), in_sp...  2.24 us
    ppermute x1, starting transfers between devices, on_device(): got_near = lax.ppermute(sends_near, ('ty', 'tx'), near)  1.56 us
    ppermute x3, waiting for transfers between devices, on_device(): lax.ppermute(chip_peaks, 'tx', [(i, i ^ m) for i in range(tx)])  1.44 us
    ppermute x1, waiting for transfers between devices, on_device(): partner = lax.ppermute(peaks, 'tx', [(i, i ^ 1) for i in range(tx)])  1.15 us
  transfers between devices with their start and end apart: 6, of which 4 were waited for; matrix products, arithmetic and copies ran while one was open for 0% of the time, Pallas kernels for 24%

profile of v5, /device:TPU:4, one launch (start us, length us, event | category | flops | bytes accessed | tf_op | source)
XLA Modules:
  0.0 19.5 jit_solution(5474972932646093699)
XLA Ops:
  0.0 1.0 %prepare.1 = (f32[96,128]{1,0:T(8,128)S(1)}, f32[96,128]{1,0:T(8,128)S(1)}, f32[4,5,8,128]{3,2,1,0:T(8,128)S(1)}, s32[4]{0:T(128)S(4)}) custom-call(s32[4]{0:T(128)} %bearing_hbm.1, s32[4]{0:T(128)} %disp_hbm.1, s32[4]{0:T(128)} %class_hbm.1, f32[128,2048]{1,0:T(8,128)} %x_ref.3), custom_call_target="tpu_custom_call" | custom-call | tf_op jit(solution)/shard_map/prepare/pallas_call | solution.py:239
  1.1 1.6 %collective-permute-start = (f32[96,128]{1,0:T(8,128)S(1)}, f32[96,128]{1,0:T(8,128)S(1)}, u32[]{:S(2)}, u32[]{:S(2)}) collective-permute-start(f32[96,128]{1,0:T(8,128)S(1)} %get-tuple-element.16), channel_id=1, source_target_pairs={{0,8},{1,9},{2,10},{3,11},{4,12},{5,13},{6,14},{7,15},{8,0},{9,1},... | collective-permute-start | bytes 147464 | tf_op jit(solution)/shard_map/ppermute | solution.py:261
  2.6 0.0 collective-permute-start.1
  2.6 2.4 %inner.1 = (f32[4,16,128,128]{3,2,1,0:T(8,128)S(1)}, f32[2,16,16,128]{3,2,1,0:T(8,128)S(1)}, f32[4,16,8,128]{3,2,1,0:T(8,128)S(1)}) custom-call(s32[4]{0:T(128)S(4)} %get-tuple-element.14.disp_ref, f32[4,5,8,128]{3,2,1,0:T(8,128)S(1)} %get-tuple-element.15.terms_ref, f32[128,2048]{1,0:T(8,128)} %x_ref.3), custom_call_target="tpu_custom_call" | custom-call | flops 41943040 | bytes 1048576 | tf_op jit(solution)/shard_map/inner/pallas_call | solution.py:263
  5.0 0.2 collective-permute-done.near_ref
  5.2 2.4 %collective-permute-done.1.far_ref = f32[96,128]{1,0:T(8,128)S(1)} collective-permute-done((f32[96,128]{1,0:T(8,128)S(1)}, f32[96,128]{1,0:T(8,128)S(1)}, u32[]{:S(2)}, u32[]{:S(2)}) %collective-permute-start.1) | collective-permute-done | bytes 49184 | tf_op jit(solution)/shard_map/ppermute | solution.py:262
  7.6 0.3 %edges.1 = (f32[4,16,128,128]{3,2,1,0:T(8,128)S(1)}, f32[4,128]{1,0:T(4,128)S(1)}) custom-call(s32[4]{0:T(128)S(4)} %get-tuple-element.14.disp_ref, f32[4,5,8,128]{3,2,1,0:T(8,128)S(1)} %get-tuple-element.15.terms_ref, f32[96,128]{1,0:T(8,128)S(1)} %collective-permute-done.near_ref, ...), custom_call_target="tpu_custom_call", output_to_operand_aliasing={{0}: (6, {})} | custom-call | tf_op jit(solution)/shard_map/edges/pallas_call | solution.py:277
  7.9 0.1 collective-permute-start.2
  8.0 1.1 %collective-permute-done.2.refs_0_ = f32[4,128]{1,0:T(4,128)S(1)} collective-permute-done((f32[4,128]{1,0:T(4,128)S(1)}, f32[4,128]{1,0:T(4,128)S(1)}, u32[]{:S(2)}, u32[]{:S(2)}) %collective-permute-start.2) | collective-permute-done | bytes 2080 | tf_op jit(solution)/shard_map/ppermute | solution.py:287
  9.1 3.6 %collective-permute-start.5 = (f32[4,128]{1,0:T(4,128)S(1)}, f32[4,128]{1,0:T(4,128)S(1)}, u32[]{:S(2)}, u32[]{:S(2)}) collective-permute-start(f32[4,128]{1,0:T(4,128)S(1)} %max.3), channel_id=1, source_target_pairs={{0,6},{1,7},{2,4},{3,5},{4,2},{5,3},{6,0},{7,1},{8,14},{9,15},{10,... | collective-permute-start | bytes 6152 | tf_op jit(solution)/shard_map/ppermute | solution.py:289
  12.7 0.0 collective-permute-start.4
  12.7 0.8 %collective-permute-start.3 = (f32[4,128]{1,0:T(4,128)S(1)}, f32[4,128]{1,0:T(4,128)S(1)}, u32[]{:S(2)}, u32[]{:S(2)}) collective-permute-start(f32[4,128]{1,0:T(4,128)S(1)} %max.3), channel_id=1, source_target_pairs={{0,2},{1,3},{2,0},{3,1},{4,6},{5,7},{6,4},{7,5},{8,10},{9,11},{10,... | collective-permute-start | bytes 6152 | tf_op jit(solution)/shard_map/ppermute | solution.py:289
  13.5 2.2 %late.1.refs_5_ = f32[4,16,128,128]{3,2,1,0:T(8,128)S(1)} custom-call(f32[4,16,128,128]{3,2,1,0:T(8,128)S(1)} %get-tuple-element.22.lifted_ref.refs_4_), custom_call_target="tpu_custom_call" | custom-call | flops 41943040 | bytes 1048576 | tf_op jit(solution)/shard_map/late/pallas_call | solution.py:290
  15.8 0.0 collective-permute-done.5.refs_3_
  15.8 1.4 %collective-permute-done.4.refs_2_ = f32[4,128]{1,0:T(4,128)S(1)} collective-permute-done((f32[4,128]{1,0:T(4,128)S(1)}, f32[4,128]{1,0:T(4,128)S(1)}, u32[]{:S(2)}, u32[]{:S(2)}) %collective-permute-start.4) | collective-permute-done | bytes 2080 | tf_op jit(solution)/shard_map/ppermute | solution.py:289
  17.2 0.0 collective-permute-done.3.refs_1_
  17.2 2.3 %finish.1 = f32[4,128,2048]{2,1,0:T(8,128)} custom-call(f32[4,128]{1,0:T(4,128)S(1)} %collective-permute-done.2.refs_0_, f32[4,128]{1,0:T(4,128)S(1)} %collective-permute-done.3.refs_1_, f32[4,128]{1,0:T(4,128)S(1)} %collective-permute-done.4.refs_2_, f32[4,128]{1,0:T(4,128)S(1)} %collective-permute-done.5.refs_3_, ...), custom_call_target="tpu_custom_call" | custom-call | tf_op jit(solution)/shard_map/finish/pallas_call | solution.py:300
  (1 shorter events, 0.0 us)
Async XLA Ops:
  1.1 4.2 %collective-permute-start = (f32[96,128]{1,0:T(8,128)S(1)}, f32[96,128]{1,0:T(8,128)S(1)}, u32[]{:S(2)}, u32[]{:S(2)}) collective-permute-start(f32[96,128]{1,0:T(8,128)S(1)} %get-tuple-element.16), channel_id=1, source_target_pairs={{0,8},{1,9},{2,10},{3,11},{4,12},{5,13},{6,14},{7,15},{8,0},{9,1},... | collective-permute-start | bytes 147464 | tf_op jit(solution)/shard_map/ppermute | solution.py:261
  2.6 5.0 %collective-permute-start.1 = (f32[96,128]{1,0:T(8,128)S(1)}, f32[96,128]{1,0:T(8,128)S(1)}, u32[]{:S(2)}, u32[]{:S(2)}) collective-permute-start(f32[96,128]{1,0:T(8,128)S(1)} %get-tuple-element.17), channel_id=1, source_target_pairs={{0,1},{1,0},{2,3},{3,2},{4,5},{5,4},{6,7},{7,6},{8,16},{9,17},{10,... | collective-permute-start | bytes 147464 | tf_op jit(solution)/shard_map/ppermute | solution.py:262
  7.9 1.2 %collective-permute-start.2 = (f32[4,128]{1,0:T(4,128)S(1)}, f32[4,128]{1,0:T(4,128)S(1)}, u32[]{:S(2)}, u32[]{:S(2)}) collective-permute-start(f32[4,128]{1,0:T(4,128)S(1)} %get-tuple-element.21), channel_id=1, source_target_pairs={{0,1},{1,0},{2,3},{3,2},{4,5},{5,4},{6,7},{7,6},{8,9},{9,8},{10,11... | collective-permute-start | bytes 6152 | tf_op jit(solution)/shard_map/ppermute | solution.py:287
  9.1 6.6 %collective-permute-start.5 = (f32[4,128]{1,0:T(4,128)S(1)}, f32[4,128]{1,0:T(4,128)S(1)}, u32[]{:S(2)}, u32[]{:S(2)}) collective-permute-start(f32[4,128]{1,0:T(4,128)S(1)} %max.3), channel_id=1, source_target_pairs={{0,6},{1,7},{2,4},{3,5},{4,2},{5,3},{6,0},{7,1},{8,14},{9,15},{10,... | collective-permute-start | bytes 6152 | tf_op jit(solution)/shard_map/ppermute | solution.py:289
  12.7 4.5 %collective-permute-start.4 = (f32[4,128]{1,0:T(4,128)S(1)}, f32[4,128]{1,0:T(4,128)S(1)}, u32[]{:S(2)}, u32[]{:S(2)}) collective-permute-start(f32[4,128]{1,0:T(4,128)S(1)} %max.3), channel_id=1, source_target_pairs={{0,4},{1,5},{2,6},{3,7},{4,0},{5,1},{6,2},{7,3},{8,12},{9,13},{10,... | collective-permute-start | bytes 6152 | tf_op jit(solution)/shard_map/ppermute | solution.py:289
  12.7 4.5 %collective-permute-start.3 = (f32[4,128]{1,0:T(4,128)S(1)}, f32[4,128]{1,0:T(4,128)S(1)}, u32[]{:S(2)}, u32[]{:S(2)}) collective-permute-start(f32[4,128]{1,0:T(4,128)S(1)} %max.3), channel_id=1, source_target_pairs={{0,2},{1,3},{2,0},{3,1},{4,6},{5,7},{6,4},{7,5},{8,10},{9,11},{10,... | collective-permute-start | bytes 6152 | tf_op jit(solution)/shard_map/ppermute | solution.py:289

commit v6 on v5

--- a/solution.py
+++ b/solution.py
@@ -158,15 +158,16 @@
         sent_ref[which : which + 1, :] = jnp.max(jnp.transpose(tall[...]), axis=0, keepdims=True)
 
 
-def late_kernel(lifted_ref, margin_ref, turned, back):
-    views, blocks, rows = lifted_ref.shape[:3]
+def late_kernel(*refs, first_view):
+    lifted_ref, margin_ref, turned, back = refs[0], *refs[-3:]
+    views, blocks, rows = margin_ref.shape[:3]
     units = [(which, j) for which in range(views) for j in range(blocks)]
     lowest = jnp.full((SUB, rows), -jnp.inf, jnp.float32)
     carried = {}
     for n in range(len(units) + 2 * DELAY):
         if n < len(units):
             which, j = units[n]
-            turned[which, j] = jnp.transpose(lifted_ref[which, j])
+            turned[which, j] = jnp.transpose(lifted_ref[first_view + which, j])
         if DELAY <= n < len(units) + DELAY:
             which, j = units[n - DELAY]
             if j == 0:
@@ -182,27 +183,31 @@
 
 
 def final_kernel(*refs, tx):
-    partner_ref, *got_refs = refs[: tx // 2]
-    lifted_ref, margin_ref, out_ref, stage, tall, sems = refs[tx // 2 :]
+    partner_ref, near_ref, *far_refs = refs[: tx // 2]
+    lifted_ref, *margin_refs, out_ref, stage, tall, sems = refs[tx // 2 :]
     views, rows, cols = out_ref.shape
     blocks, tiles = cols // LANE, rows // SUB
     place = lax.axis_index("tx")
-    chip = place // 2
-    before = jnp.where(lax.rem(place, 2) == 1, partner_ref[...], -jnp.inf)
-    for i, got_ref in enumerate(got_refs):
-        before = jnp.maximum(before, jnp.where((chip ^ (i + 1)) < chip, got_ref[...], -jnp.inf))
+    chip, core = place // 2, lax.rem(place, 2)
+    before = jnp.where(core == 1, partner_ref[...], -jnp.inf)
+    got = [(1, near_ref)]
+    for i in range(0, len(far_refs), 2):
+        got += [(2 + i + core, far_refs[i]), (3 + i - core, far_refs[i + 1])]
+    for offset, got_ref in got:
+        before = jnp.maximum(before, jnp.where((chip ^ offset) < chip, got_ref[...], -jnp.inf))
     for which in range(views):
         tall[which] = jnp.transpose(jnp.broadcast_to(before[which : which + 1, :], (LANE, rows)))
     chunk = rows // CHUNKS
     copies = []
     for which in range(views):
+        margin_ref = margin_refs[which // (views // len(margin_refs))].at[which % (views // len(margin_refs))]
         for first in range(0, rows, chunk):
             for t in range(first, first + chunk, SUB):
                 span = slice(t, t + SUB)
                 top = tall[which, span, :]
                 for j in range(blocks):
                     stage[which, span, j * LANE : (j + 1) * LANE] = jnp.maximum(
-                        margin_ref[which, j, span, :], top - lifted_ref[which, j, span, :]
+                        margin_ref[j, span, :], top - lifted_ref[which, j, span, :]
                     )
             part = pl.ds(first, chunk)
             copies.append(
@@ -229,7 +234,7 @@
     views = bearing.shape[0]
     tiles, blocks = rows // SUB, cols // LANE
     f32 = jnp.float32
-    assert tx & (tx - 1) == 0 and tx > 1 and ty % 2 == 0
+    assert tx & (tx - 1) == 0 and tx > 4 and ty % 2 == 0
     smem = pl.BlockSpec(memory_space=pltpu.SMEM)
     vmem = pl.BlockSpec(memory_space=pltpu.VMEM)
     hbm = pl.BlockSpec(memory_space=pltpu.HBM)
@@ -284,23 +289,35 @@
         input_output_aliases={6: 0},
         name="edges",
     )(shifts, terms, got_near, got_far, edge, peak, lifted)
-    partner = lax.ppermute(peaks, "tx", [(i, i ^ 1) for i in range(tx)])
+    swap = [(i, i ^ 1) for i in range(tx)]
+    partner = lax.ppermute(peaks, "tx", swap)
     chip_peaks = jnp.maximum(peaks, partner)
-    got = [lax.ppermute(chip_peaks, "tx", [(i, i ^ m) for i in range(tx)]) for m in range(2, tx, 2)]
-    margin = pl.pallas_call(
-        late_kernel,
-        out_shape=pltpu.VMEM(block_shape, f32),
-        in_specs=[vmem],
-        out_specs=vmem,
-        scratch_shapes=[pltpu.VMEM((views, blocks, LANE, rows), f32)] * 2,
-        compiler_params=pltpu.CompilerParams(vmem_limit_bytes=24 * MIB),
-        cost_estimate=pl.CostEstimate(flops=views * rows * cols * 40, bytes_accessed=rows * cols * 4, transcendentals=0),
-        name="late",
-    )(lifted)
+    far = [
+        lax.ppermute(chip_peaks, "tx", [(i, i ^ 2 * (2 * m + i % 2)) for i in range(tx)])
+        for m in range(1, tx // 4)
+    ]
+    near = lax.ppermute(chip_peaks, "tx", [(i, i ^ 2) for i in range(tx)])
+    got = [near]
+    for part in far:
+        got += [part, lax.ppermute(part, "tx", swap)]
+    margins = []
+    for half in range(2):
+        margins.append(
+            pl.pallas_call(
+                functools.partial(late_kernel, first_view=half * (views // 2)),
+                out_shape=pltpu.VMEM((views // 2,) + block_shape[1:], f32),
+                in_specs=[vmem] * (1 + half * len(far)),
+                out_specs=vmem,
+                scratch_shapes=[pltpu.VMEM((views // 2, blocks, LANE, rows), f32)] * 2,
+                compiler_params=pltpu.CompilerParams(vmem_limit_bytes=16 * MIB),
+                cost_estimate=pl.CostEstimate(flops=views * rows * cols * 20, bytes_accessed=rows * cols * 2, transcendentals=0),
+                name="late",
+            )(lifted, *far[: half * len(far)])
+        )
     return pl.pallas_call(
         functools.partial(final_kernel, tx=tx),
         out_shape=jax.ShapeDtypeStruct((views, rows, cols), f32),
-        in_specs=[vmem] * (tx // 2 + 2),
+        in_specs=[vmem] * (tx // 2 + 3),
         out_specs=hbm,
         scratch_shapes=[
             pltpu.VMEM((views, rows, cols), f32),
@@ -309,7 +326,7 @@
         ],
         compiler_params=pltpu.CompilerParams(vmem_limit_bytes=16 * MIB),
         name="finish",
-    )(partner, *got, lifted, margin)
+    )(partner, *got, lifted, *margins)
 
 
 def solution(mesh):

time: 19.7 us -> 19 us (0.964)
  waiting for transfers between devices: 5.17 us -> 4.44 us
  Pallas kernels: 8.22 us -> 8.44 us
    ppermute x4, waiting for transfers between devices: 2.59 us -> 1.98 us  [the longest x1 1.15 us: on_device(): partner = lax.ppermute(peaks, 'tx', swap)]
    pallas_call x1 -> x2, Pallas kernels: 2.24 us -> 2.34 us  [on_device(): pl.pallas_call(functools.partial(late_kernel, first_view=half * (views //...]
  transfers between devices with their start and end apart: 6 -> 6, of which waited for: 4 -> 4; matrix products, arithmetic and copies ran while one was open for 0% -> 0% of each run, Pallas kernels for 24% -> 26%
where the time goes in v6:
time: 19 us; the launch traced here: 18.8 us
  Pallas kernels  8.44 us (44%)
  starting transfers between devices  5.88 us (31%)
  waiting for transfers between devices  4.44 us (23%)
    ppermute x1, starting transfers between devices, on_device(): lax.ppermute(chip_peaks, 'tx', [(i, i ^ 2 * (2 * m + i % 2)) for i in ran...  2.59 us
    pallas_call x1, Pallas kernels, on_device(): pl.pallas_call(inner_kernel, out_shape=(pltpu.VMEM(block_shape, f32), plt...  2.5 us
    ppermute x1, waiting for transfers between devices, on_device(): got_far = lax.ppermute(sends_far, ('ty', 'tx'), far)  2.39 us
    pallas_call x2, Pallas kernels, on_device(): pl.pallas_call(functools.partial(late_kernel, first_view=half * (views //...  2.34 us
    pallas_call x1, Pallas kernels, on_device(): pl.pallas_call(functools.partial(final_kernel, tx=tx), out_shape=jax.Shap...  2.26 us
    ppermute x1, starting transfers between devices, on_device(): near = lax.ppermute(chip_peaks, 'tx', [(i, i ^ 2) for i in range(tx)])  1.64 us
    ppermute x1, starting transfers between devices, on_device(): got_near = lax.ppermute(sends_near, ('ty', 'tx'), near)  1.56 us
    ppermute x1, waiting for transfers between devices, on_device(): partner = lax.ppermute(peaks, 'tx', swap)  1.15 us
  transfers between devices with their start and end apart: 6, of which 4 were waited for; matrix products, arithmetic and copies ran while one was open for 0% of the time, Pallas kernels for 26%

profile of v6, /device:TPU:4, one launch (start us, length us, event | category | flops | bytes accessed | tf_op | source)
XLA Modules:
  0.0 18.8 jit_solution(2906626991006455855)
XLA Ops:
  0.0 1.0 %prepare.1 = (f32[96,128]{1,0:T(8,128)S(1)}, f32[96,128]{1,0:T(8,128)S(1)}, f32[4,5,8,128]{3,2,1,0:T(8,128)S(1)}, s32[4]{0:T(128)S(4)}) custom-call(s32[4]{0:T(128)} %bearing_hbm.1, s32[4]{0:T(128)} %disp_hbm.1, s32[4]{0:T(128)} %class_hbm.1, f32[128,2048]{1,0:T(8,128)} %x_ref.3), custom_call_target="tpu_custom_call" | custom-call | tf_op jit(solution)/shard_map/prepare/pallas_call | solution.py:244
  1.1 1.6 %collective-permute-start = (f32[96,128]{1,0:T(8,128)S(1)}, f32[96,128]{1,0:T(8,128)S(1)}, u32[]{:S(2)}, u32[]{:S(2)}) collective-permute-start(f32[96,128]{1,0:T(8,128)S(1)} %get-tuple-element.16), channel_id=1, source_target_pairs={{0,8},{1,9},{2,10},{3,11},{4,12},{5,13},{6,14},{7,15},{8,0},{9,1},... | collective-permute-start | bytes 147464 | tf_op jit(solution)/shard_map/ppermute | solution.py:266
  2.6 0.0 collective-permute-start.1
  2.6 2.5 %inner.1 = (f32[4,16,128,128]{3,2,1,0:T(8,128)S(1)}, f32[2,16,16,128]{3,2,1,0:T(8,128)S(1)}, f32[4,16,8,128]{3,2,1,0:T(8,128)S(1)}) custom-call(s32[4]{0:T(128)S(4)} %get-tuple-element.14.disp_ref, f32[4,5,8,128]{3,2,1,0:T(8,128)S(1)} %get-tuple-element.15.terms_ref, f32[128,2048]{1,0:T(8,128)} %x_ref.3), custom_call_target="tpu_custom_call" | custom-call | flops 41943040 | bytes 1048576 | tf_op jit(solution)/shard_map/inner/pallas_call | solution.py:268
  5.1 0.1 collective-permute-done.near_ref
  5.2 2.4 %collective-permute-done.1.far_ref = f32[96,128]{1,0:T(8,128)S(1)} collective-permute-done((f32[96,128]{1,0:T(8,128)S(1)}, f32[96,128]{1,0:T(8,128)S(1)}, u32[]{:S(2)}, u32[]{:S(2)}) %collective-permute-start.1) | collective-permute-done | bytes 49184 | tf_op jit(solution)/shard_map/ppermute | solution.py:267
  7.6 0.3 %edges.1 = (f32[4,16,128,128]{3,2,1,0:T(8,128)S(1)}, f32[4,128]{1,0:T(4,128)S(1)}) custom-call(s32[4]{0:T(128)S(4)} %get-tuple-element.14.disp_ref, f32[4,5,8,128]{3,2,1,0:T(8,128)S(1)} %get-tuple-element.15.terms_ref, f32[96,128]{1,0:T(8,128)S(1)} %collective-permute-done.near_ref, ...), custom_call_target="tpu_custom_call", output_to_operand_aliasing={{0}: (6, {})} | custom-call | tf_op jit(solution)/shard_map/edges/pallas_call | solution.py:282
  7.9 0.1 collective-permute-start.2
  8.0 1.1 %collective-permute-done.2.refs_0_ = f32[4,128]{1,0:T(4,128)S(1)} collective-permute-done((f32[4,128]{1,0:T(4,128)S(1)}, f32[4,128]{1,0:T(4,128)S(1)}, u32[]{:S(2)}, u32[]{:S(2)}) %collective-permute-start.2) | collective-permute-done | bytes 2080 | tf_op jit(solution)/shard_map/ppermute | solution.py:293
  9.1 2.6 %collective-permute-start.4 = (f32[4,128]{1,0:T(4,128)S(1)}, f32[4,128]{1,0:T(4,128)S(1)}, u32[]{:S(2)}, u32[]{:S(2)}) collective-permute-start(f32[4,128]{1,0:T(4,128)S(1)} %max.3), channel_id=1, source_target_pairs={{0,4},{1,7},{2,6},{3,5},{4,0},{5,3},{6,2},{7,1},{8,12},{9,15},{10,... | collective-permute-start | bytes 6152 | tf_op jit(solution)/shard_map/ppermute | solution.py:296
  11.7 1.2 %late.2.refs_5_ = f32[2,16,128,128]{3,2,1,0:T(8,128)S(1)} custom-call(f32[4,16,128,128]{3,2,1,0:T(8,128)S(1)} %get-tuple-element.22.refs_0_.refs_4_), custom_call_target="tpu_custom_call" | custom-call | flops 20971520 | bytes 524288 | tf_op jit(solution)/shard_map/late/pallas_call | solution.py:306
  12.9 1.6 %collective-permute-start.3 = (f32[4,128]{1,0:T(4,128)S(1)}, f32[4,128]{1,0:T(4,128)S(1)}, u32[]{:S(2)}, u32[]{:S(2)}) collective-permute-start(f32[4,128]{1,0:T(4,128)S(1)} %max.3), channel_id=1, source_target_pairs={{0,2},{1,3},{2,0},{3,1},{4,6},{5,7},{6,4},{7,5},{8,10},{9,11},{10,... | collective-permute-start | bytes 6152 | tf_op jit(solution)/shard_map/ppermute | solution.py:299
  14.5 0.0 collective-permute-done.4.refs_1_.refs_2_
  14.5 0.0 collective-permute-start.5
  14.5 1.2 %late.3.refs_6_ = f32[2,16,128,128]{3,2,1,0:T(8,128)S(1)} custom-call(f32[4,16,128,128]{3,2,1,0:T(8,128)S(1)} %get-tuple-element.22.refs_0_.refs_4_, f32[4,128]{1,0:T(4,128)S(1)} %collective-permute-done.4.refs_1_.refs_2_), custom_call_target="tpu_custom_call" | custom-call | flops 20971520 | bytes 524288 | tf_op jit(solution)/shard_map/late/pallas_call | solution.py:306
  15.7 0.8 %collective-permute-done.3.refs_1_ = f32[4,128]{1,0:T(4,128)S(1)} collective-permute-done((f32[4,128]{1,0:T(4,128)S(1)}, f32[4,128]{1,0:T(4,128)S(1)}, u32[]{:S(2)}, u32[]{:S(2)}) %collective-permute-start.3) | collective-permute-done | bytes 2080 | tf_op jit(solution)/shard_map/ppermute | solution.py:299
  16.5 0.0 collective-permute-done.5.refs_3_
  16.5 2.3 %finish.1 = f32[4,128,2048]{2,1,0:T(8,128)} custom-call(f32[4,128]{1,0:T(4,128)S(1)} %collective-permute-done.2.refs_0_, f32[4,128]{1,0:T(4,128)S(1)} %collective-permute-done.3.refs_1_, f32[4,128]{1,0:T(4,128)S(1)} %collective-permute-done.4.refs_1_.refs_2_, f32[4,128]{1,0:T(4,128)S(1)} %collective-permute-done.5.refs_3_, ...), custom_call_target="tpu_custom_call" | custom-call | tf_op jit(solution)/shard_map/finish/pallas_call | solution.py:317
  (1 shorter events, 0.0 us)
Async XLA Ops:
  1.1 4.2 %collective-permute-start = (f32[96,128]{1,0:T(8,128)S(1)}, f32[96,128]{1,0:T(8,128)S(1)}, u32[]{:S(2)}, u32[]{:S(2)}) collective-permute-start(f32[96,128]{1,0:T(8,128)S(1)} %get-tuple-element.16), channel_id=1, source_target_pairs={{0,8},{1,9},{2,10},{3,11},{4,12},{5,13},{6,14},{7,15},{8,0},{9,1},... | collective-permute-start | bytes 147464 | tf_op jit(solution)/shard_map/ppermute | solution.py:266
  2.6 5.0 %collective-permute-start.1 = (f32[96,128]{1,0:T(8,128)S(1)}, f32[96,128]{1,0:T(8,128)S(1)}, u32[]{:S(2)}, u32[]{:S(2)}) collective-permute-start(f32[96,128]{1,0:T(8,128)S(1)} %get-tuple-element.17), channel_id=1, source_target_pairs={{0,1},{1,0},{2,3},{3,2},{4,5},{5,4},{6,7},{7,6},{8,16},{9,17},{10,... | collective-permute-start | bytes 147464 | tf_op jit(solution)/shard_map/ppermute | solution.py:267
  7.9 1.2 %collective-permute-start.2 = (f32[4,128]{1,0:T(4,128)S(1)}, f32[4,128]{1,0:T(4,128)S(1)}, u32[]{:S(2)}, u32[]{:S(2)}) collective-permute-start(f32[4,128]{1,0:T(4,128)S(1)} %get-tuple-element.21), channel_id=1, source_target_pairs={{0,1},{1,0},{2,3},{3,2},{4,5},{5,4},{6,7},{7,6},{8,9},{9,8},{10,11... | collective-permute-start | bytes 6152 | tf_op jit(solution)/shard_map/ppermute | solution.py:293
  9.1 5.4 %collective-permute-start.4 = (f32[4,128]{1,0:T(4,128)S(1)}, f32[4,128]{1,0:T(4,128)S(1)}, u32[]{:S(2)}, u32[]{:S(2)}) collective-permute-start(f32[4,128]{1,0:T(4,128)S(1)} %max.3), channel_id=1, source_target_pairs={{0,4},{1,7},{2,6},{3,5},{4,0},{5,3},{6,2},{7,1},{8,12},{9,15},{10,... | collective-permute-start | bytes 6152 | tf_op jit(solution)/shard_map/ppermute | solution.py:296
  12.9 3.7 %collective-permute-start.3 = (f32[4,128]{1,0:T(4,128)S(1)}, f32[4,128]{1,0:T(4,128)S(1)}, u32[]{:S(2)}, u32[]{:S(2)}) collective-permute-start(f32[4,128]{1,0:T(4,128)S(1)} %max.3), channel_id=1, source_target_pairs={{0,2},{1,3},{2,0},{3,1},{4,6},{5,7},{6,4},{7,5},{8,10},{9,11},{10,... | collective-permute-start | bytes 6152 | tf_op jit(solution)/shard_map/ppermute | solution.py:299
  14.5 2.0 %collective-permute-start.5 = (f32[4,128]{1,0:T(4,128)S(1)}, f32[4,128]{1,0:T(4,128)S(1)}, u32[]{:S(2)}, u32[]{:S(2)}) collective-permute-start(f32[4,128]{1,0:T(4,128)S(1)} %collective-permute-done.4.refs_1_.refs_2_), channel_id=1, source_target_pairs={{0,1},{1,0},{2,3},{3,2},{4,5},{5,4},{6,7},{7,6},{8,9},{9,8},{10,11... | collective-permute-start | bytes 6152 | tf_op jit(solution)/shard_map/ppermute | solution.py:302
